TPU v7x, 16 devices: a 4x2x1 block of a 4x4x8 slice. The times are simulated.
16 devices in a mesh: replica: 2 (over y, z), ep: 8 (over x, core).
Axes of the slice: x: 4, y: 2, z: 1, core: 2. Of those that a mesh axis runs over, the one named last changes fastest.
The devices are a block of a 4x4x8 slice.
Arguments:
- tok_in: bfloat16 [8192, 2048], P(('replica', 'ep')), parts along dimension 0
- routes: int32 [2, 8192, 8], P(None, ('replica', 'ep')), parts along dimension 1
- gate_vals: float32 [2, 8192, 8], P(None, ('replica', 'ep')), parts along dimension 1
- w_gate: bfloat16 [2, 32, 2048, 768], P(None, ('replica', 'ep')), parts along dimension 1
- w_up: bfloat16 [2, 32, 2048, 768], P(None, ('replica', 'ep')), parts along dimension 1
- w_down: bfloat16 [2, 32, 768, 2048], P(None, ('replica', 'ep')), parts along dimension 1
- sh_gate: bfloat16 [2, 2048, 768], replicated
- sh_up: bfloat16 [2, 2048, 768], replicated
- sh_down: bfloat16 [2, 768, 2048], replicated
- old_map: int32 [2, 32], P(None, 'replica'), parts along dimension 1
- move_slot: int32 [2, 4], P(None, 'replica'), parts along dimension 1
- move_expert: int32 [2, 4], P(None, 'replica'), parts along dimension 1
Outputs:
- output 1: bfloat16 [8192, 2048], P(('replica', 'ep')), parts along dimension 0
- output 2: bfloat16 [2, 32, 2048, 768], P(None, ('replica', 'ep')), parts along dimension 1
- output 3: bfloat16 [2, 32, 2048, 768], P(None, ('replica', 'ep')), parts along dimension 1
- output 4: bfloat16 [2, 32, 768, 2048], P(None, ('replica', 'ep')), parts along dimension 1
There are 2 independent parts. A program takes and returns all parts, laid end to end along the dimension named above; an argument that names none is the same for every part.
All inputs are finite; a program needn't handle non-finite values.
Results may differ from a plain program's by a relative error of at most 0.0115771.
Values are sent between devices in bfloat16 or wider.
A program may use at most 768 MiB of HBM per device.

v0:
```python
import jax
import jax.numpy as jnp
from jax import lax
from jax.sharding import PartitionSpec as P

TOKEN_AXES = ('replica', 'ep')


def first_holder(slot_map, wanted):
    slot_ids = jnp.arange(slot_map.shape[0], dtype=jnp.int32)
    hit_mask = slot_map[None, :] == wanted[:, None]
    return jnp.min(jnp.where(hit_mask, slot_ids[None, :], slot_map.shape[0]), axis=1)


def swiglu(hidden, w_gate, w_up, w_down):
    gate_proj = jnp.dot(hidden, w_gate, preferred_element_type=jnp.float32)
    up_proj = jnp.dot(hidden, w_up, preferred_element_type=jnp.float32)
    inner_act = (jax.nn.silu(gate_proj) * up_proj).astype(jnp.bfloat16)
    return jnp.dot(inner_act, w_down, preferred_element_type=jnp.float32)


def send_moved(weights, slot_map, move_expert, slots_dev, my_dev):
    source = first_holder(slot_map, move_expert)
    is_source = (source // slots_dev) == my_dev
    local_idx = source % slots_dev
    return tuple(jnp.where(is_source[:, None, None], jnp.take(weight_arr, local_idx, axis=0), jnp.zeros((), weight_arr.dtype)) for weight_arr in weights)


def place_moved(weights, arrived, move_slot, slots_dev, my_dev):
    local_ids = my_dev * slots_dev + jnp.arange(slots_dev, dtype=jnp.int32)
    match_mask = (move_slot[None, :] == local_ids[:, None]).astype(jnp.int32)
    is_target = jnp.max(match_mask, axis=1) > 0
    pick_idx = jnp.argmax(match_mask, axis=1)
    return tuple(jnp.where(is_target[:, None, None], jnp.take(arrived_arr, pick_idx, axis=0), weight_arr) for arrived_arr, weight_arr in zip(arrived, weights))


def moe_layer(hidden, route_all, gate_all, expert_w, shared_w, slot_map, slots_dev, my_dev):
    gathered = lax.all_gather(hidden, 'ep', axis=0, tiled=True)
    slot_ids = jnp.arange(slot_map.shape[0], dtype=jnp.int32)
    serve_all = (first_holder(slot_map, slot_map) == slot_ids).astype(jnp.float32)
    local_map = lax.dynamic_slice_in_dim(slot_map, my_dev * slots_dev, slots_dev)
    local_serve = lax.dynamic_slice_in_dim(serve_all, my_dev * slots_dev, slots_dev)
    hit_mask = route_all[:, :, None] == local_map[None, None, :]
    gate_coef = jnp.sum(jnp.where(hit_mask, gate_all[:, :, None], 0.0), axis=1) * local_serve[None, :]
    gate_proj = jnp.einsum('nd,jdf->jnf', gathered, expert_w[0], preferred_element_type=jnp.float32)
    up_proj = jnp.einsum('nd,jdf->jnf', gathered, expert_w[1], preferred_element_type=jnp.float32)
    inner_act = (jax.nn.silu(gate_proj) * up_proj).astype(jnp.bfloat16)
    expert_out = jnp.einsum('jnf,jfd->jnd', inner_act, expert_w[2], preferred_element_type=jnp.float32)
    partial_sum = jnp.sum(expert_out * gate_coef.T[:, :, None], axis=0)
    combined = lax.psum_scatter(partial_sum, 'ep', scatter_dimension=0, tiled=True)
    shared_out = swiglu(hidden, shared_w[0], shared_w[1], shared_w[2])
    return (hidden.astype(jnp.float32) + shared_out + combined).astype(jnp.bfloat16)


def solution(mesh):
    def body(tok_in, routes, gate_vals, w_gate, w_up, w_down, sh_gate, sh_up, sh_down, old_map, move_slot, move_expert):
        my_dev = lax.axis_index('ep')
        slots_dev = w_gate.shape[1]
        route_all = lax.all_gather(routes, 'ep', axis=1, tiled=True)
        gate_all = lax.all_gather(gate_vals, 'ep', axis=1, tiled=True)
        hidden = tok_in
        placed = []
        for layer_idx in range(2):
            layer_w = (w_gate[layer_idx], w_up[layer_idx], w_down[layer_idx])
            outgoing = send_moved(layer_w, old_map[layer_idx], move_expert[layer_idx], slots_dev, my_dev)
            arrived = lax.psum(outgoing, 'ep')
            new_w = place_moved(layer_w, arrived, move_slot[layer_idx], slots_dev, my_dev)
            new_map = old_map[layer_idx].at[move_slot[layer_idx]].set(move_expert[layer_idx])
            shared_w = (sh_gate[layer_idx], sh_up[layer_idx], sh_down[layer_idx])
            hidden = moe_layer(hidden, route_all[layer_idx], gate_all[layer_idx], new_w, shared_w, new_map, slots_dev, my_dev)
            placed.append(new_w)
        new_gate = jnp.stack([placed[0][0], placed[1][0]])
        new_up = jnp.stack([placed[0][1], placed[1][1]])
        new_down = jnp.stack([placed[0][2], placed[1][2]])
        return (hidden, new_gate, new_up, new_down)

    weight_spec = P(None, TOKEN_AXES, None, None)
    route_spec = P(None, TOKEN_AXES, None)
    map_spec = P(None, 'replica')
    shared_spec = P(None, None, None)
    tok_spec = P(TOKEN_AXES, None)
    return jax.shard_map(body, mesh=mesh, in_specs=(tok_spec, route_spec, route_spec, weight_spec, weight_spec, weight_spec, shared_spec, shared_spec, shared_spec, map_spec, map_spec, map_spec), out_specs=(tok_spec, weight_spec, weight_spec, weight_spec), check_vma=False)
```

profile of v0, /device:TPU:112, one launch (start us, length us, event | category | flops | bytes accessed | tf_op | source)
XLA Modules:
  0.0 1299.0 jit_solution(10724408515292066935)
XLA Ops:
  8.8 5.3 slice_bitcast_fusion.3
  24.9 5.3 slice_bitcast_fusion.2
  30.2 4.7 fusion.92
  37.5 4.3 gather_fusion.12
  41.8 5.3 slice_bitcast_fusion.4
  47.1 4.7 fusion.94
  56.1 4.3 gather_fusion.16
  60.5 4.4 gather_fusion.9
  64.8 4.3 gather_fusion.8
  69.2 4.3 gather_fusion.1
  73.5 4.3 gather_fusion
  77.8 4.4 gather_fusion.5
  86.4 8.1 fusion.38
  94.5 6.4 fusion.34
  107.8 6.4 fusion.28
  116.7 24.9 %all_gather.14 = f32[2,4096,8]{1,2,0:T(8,128)S(1)} all-gather(f32[2,512,8]{1,2,0:T(8,128)S(1)} %copy-done.18), channel_id=1, replica_groups=mesh['replica'=2,'ep'=8] {'ep'}, dimensions={1}, use_global_device_ids=true | all-gather | bytes 294912 | tf_op jit(solution)/shard_map/all_gather | solution.py:60
  141.6 22.0 %all_gather.13 = s32[2,4096,8]{1,2,0:T(8,128)S(1)} all-gather(s32[2,512,8]{1,2,0:T(8,128)S(1)} %copy-done.19), channel_id=1, replica_groups=mesh['replica'=2,'ep'=8] {'ep'}, dimensions={1}, use_global_device_ids=true | all-gather | bytes 294912 | tf_op jit(solution)/shard_map/all_gather | solution.py:59
  167.4 324.3 %all-reduce.3.cloned.1.call-done = (bf16[2,768,2048]{2,1,0:T(8,128)(2,1)}, bf16[2,2048,768]{2,1,0:T(8,128)(2,1)}, bf16[2,768,2048]{2,1,0:T(8,128)(2,1)}, bf16[2,...) async-done(((bf16[2,768,2048]{2,1,0:T(8,128)(2,1)}, bf16[2,2048,768]{2,1,0:T(8,128)(2,1)}, bf16[2,768,2048]{2,1,0:T(8,128)(2,1)}, ...) | async-done | bytes 37748752 | tf_op jit(solution)/shard_map/psum | solution.py:66
  491.7 5.6 fusion.89
  497.3 4.3 gather_fusion.11
  504.0 5.6 fusion.91
  509.6 4.3 gather_fusion.23
  516.4 5.9 fusion.88
  524.9 4.4 gather_fusion.6
  529.3 5.9 fusion.90
  535.2 4.3 gather_fusion.19
  543.8 5.9 fusion.87
  549.7 4.4 gather_fusion.3
  554.1 4.3 gather_fusion.2
  558.4 5.9 fusion.86
  568.6 4.3 gather_fusion.14
  572.9 17.6 %fusion.33 = (bf16[2,768,2048]{2,1,0:T(8,128)(2,1)}, bf16[2,768,2048]{2,1,0:T(8,128)(2,1)}) fusion(bf16[2,768,1024]{2,1,0:T(8,128)(2,1)} %gather_fusion.11, bf16[2,768,1024]{2,1,0:T(8,128)(2,1)} %gather_fusion.10, pred[2]{0:T(512)(128)(4,1)S(1)} %get-tuple-element.89, pred[2]{0:T(512)(128)(4,1)S(1)} %get-tuple-element.87, ...), kind=kLoop, calls=%fused_computation.66 | loop fusion | flops 37748736 | bytes 37748744 | tf_op jit(solution)/shard_map/jit(_where)/select_n | solution.py:34
  590.5 22.8 %fusion.31 = (bf16[2,2048,768]{2,1,0:T(8,128)(2,1)}, bf16[2,2048,768]{2,1,0:T(8,128)(2,1)}, bf16[2,2048,768]{2,1,0:T(8,128)(2,1)}, bf16[2,2048,768]{2,1,0:T(8,128)(2,1)}) fusion(bf16[2,1024,768]{2,1,0:T(8,128)(2,1)S(1)} %gather_fusion.7, bf16[2,1024,768]{2,1,0:T(8,128)(2,1)S(1)} %copy-done.3, pred[2]{0:T(512)(128)(4,1)S(1)} %get-tuple-element.89, ...), kind=kLoop, calls=%fused_computation.62 | loop fusion | flops 75497472 | bytes 75497480 | tf_op jit(solution)/shard_map/jit(_where)/select_n | solution.py:34
  613.4 34.2 %fusion.12 = f32[2,768,4096]{2,1,0:T(8,128)} fusion(bf16[2,2048,768]{2,1,0:T(8,128)(2,1)} %get-tuple-element.24, bf16[4096,2048]{1,0:T(8,128)(2,1)} %all-gather.3.cloned.1.call-done), kind=kOutput, calls=%fused_computation.46 | convolution fusion | flops 25769803776 | bytes 48234496 | tf_op jit(solution)/shard_map/nd,jdf->jnf/dot_general | solution.py:46
  647.6 39.6 %fusion.121 = bf16[2,4096,768]{1,2,0:T(8,128)(2,1)} fusion(f32[2,768,4096]{2,1,0:T(8,128)} %fusion.12, bf16[2,2048,768]{2,1,0:T(8,128)(2,1)S(1)} %copy-done.2, bf16[4096,2048]{1,0:T(8,128)(2,1)} %all-gather.3.cloned.1.call-done), kind=kOutput, calls=%fused_computation.36.clone.clone | convolution fusion | flops 25807552512 | bytes 60817408 | tf_op jit(solution)/shard_map/nd,jdf->jnf/dot_general | solution.py:45
  687.2 47.7 %multiply_reduce_fusion.1 = f32[4096,2048]{1,0:T(8,128)} fusion(f32[2,4096]{1,0:T(2,128)S(1)} %copy-done.20, bf16[2,768,2048]{2,1,0:T(8,128)(2,1)} %get-tuple-element.26, bf16[2,4096,768]{1,2,0:T(8,128)(2,1)} %fusion.121), kind=kOutput, calls=%fused_computation.27 | convolution fusion | flops 25794969600 | bytes 52461568 | tf_op jit(solution)/shard_map/jnf,jfd->jnd/dot_general | solution.py:48
  736.5 4.8 fusion.50
  741.4 160.1 %reduce-scatter.3.cloned.1.call-done = f32[512,2048]{1,0:T(8,128)} async-done(((f32[4096,2048]{1,0:T(8,128)}), f32[512,2048]{1,0:T(8,128)}) %reduce-scatter.3.cloned.1.call-update) | async-done | bytes 4194320 | tf_op jit(solution)/shard_map/reduce_scatter | solution.py:50
  901.4 11.1 add_convert_fusion.1
  913.9 79.7 %all-gather.5.cloned.1.call-done = bf16[4096,2048]{1,0:T(8,128)(2,1)} async-done(((bf16[512,2048]{1,0:T(8,128)(2,1)}), bf16[4096,2048]{1,0:T(8,128)(2,1)}) %all-gather.5.cloned.1.call-update) | async-done | bytes 16777232 | tf_op jit(solution)/shard_map/all_gather | solution.py:38
  993.5 34.1 %fusion.8 = f32[2,768,4096]{2,1,0:T(8,128)} fusion(bf16[2,2048,768]{2,1,0:T(8,128)(2,1)} %get-tuple-element.25, bf16[4096,2048]{1,0:T(8,128)(2,1)} %all-gather.5.cloned.1.call-done), kind=kOutput, calls=%fused_computation.42 | convolution fusion | flops 25769803776 | bytes 48234496 | tf_op jit(solution)/shard_map/nd,jdf->jnf/dot_general | solution.py:46
  1027.7 39.5 %fusion.117 = bf16[2,4096,768]{1,2,0:T(8,128)(2,1)} fusion(f32[2,768,4096]{2,1,0:T(8,128)} %fusion.8, bf16[2,2048,768]{2,1,0:T(8,128)(2,1)S(1)} %bitcast.192, bf16[4096,2048]{1,0:T(8,128)(2,1)} %all-gather.5.cloned.1.call-done), kind=kOutput, calls=%fused_computation.29.clone.clone.1 | convolution fusion | flops 25807552512 | bytes 60817408 | tf_op jit(solution)/shard_map/nd,jdf->jnf/dot_general | solution.py:45
  1067.2 47.8 %multiply_reduce_fusion = f32[4096,2048]{1,0:T(8,128)} fusion(f32[2,4096]{1,0:T(2,128)S(1)} %multiply_bitcast_fusion, bf16[2,768,2048]{2,1,0:T(8,128)(2,1)} %get-tuple-element.27, bf16[2,4096,768]{1,2,0:T(8,128)(2,1)} %fusion.117), kind=kOutput, calls=%fused_computation.26 | convolution fusion | flops 25794969600 | bytes 52461568 | tf_op jit(solution)/shard_map/jnf,jfd->jnd/dot_general | solution.py:48
  1115.1 12.3 pad_maximum_fusion
  1127.6 6.3 pad_maximum_fusion.1
  1136.3 5.7 pad_maximum_fusion.2
  1145.1 137.1 %reduce-scatter.5.cloned.1.call-done = f32[512,2048]{1,0:T(8,128)} async-done(((f32[4096,2048]{1,0:T(8,128)}), f32[512,2048]{1,0:T(8,128)}) %reduce-scatter.5.cloned.1.call-update) | async-done | bytes 4194320 | tf_op jit(solution)/shard_map/reduce_scatter | solution.py:50
  1282.1 9.8 add_convert_fusion
  (139 shorter events, 61.2 us)
Async XLA Ops:
  7.2 484.6 %all-reduce.3.cloned.1.call-start = ((), (), s32[]{:S(2)}) async-start(), calls=%async_computation.6 | async-start | bytes 75497472 | tf_op jit(solution)/shard_map/psum | solution.py:66
  8.0 6.1 copy-start
  8.8 5.3 copy-start.21
  86.4 8.1 copy-start.5
  86.4 8.1 copy-start.6
  86.4 8.1 copy-start.7
  94.5 6.4 copy-start.12
  94.5 6.4 copy-start.13
  100.9 4.0 copy-start.8
  100.9 5.1 copy-start.9
  100.9 6.0 copy-start.10
  100.9 6.8 copy-start.11
  114.2 1.0 copy-start.23
  114.2 2.5 copy-start.18
  114.2 27.4 %copy-start.19 = (s32[2,512,8]{1,2,0:T(8,128)S(1)}, s32[2,512,8]{1,2,0:T(8,128)}, u32[]{:S(2)}) copy-start(s32[2,512,8]{1,2,0:T(8,128)} %param.17) | copy-start | bytes 98308
  114.2 499.1 %all-gather.3.cloned.1.call-start = ((), (), s32[]{:S(2)}) async-start(), calls=%async_computation.2 | async-start | bytes 18874368 | tf_op jit(solution)/shard_map/all_gather | solution.py:38
  115.1 786.4 %reduce-scatter.3.cloned.1.call-start = ((), (), s32[]{:S(2)}) async-start(), calls=%async_computation.3 | async-start | bytes 37748736 | tf_op jit(solution)/shard_map/reduce_scatter | solution.py:50
  572.9 17.6 %copy-start.3 = (bf16[2,1024,768]{2,1,0:T(8,128)(2,1)S(1)}, bf16[2,1024,768]{2,1,0:T(8,128)(2,1)}, u32[]{:S(2)}) copy-start(bf16[2,1024,768]{2,1,0:T(8,128)(2,1)} %gather_fusion.6) | copy-start | bytes 9437188
  572.9 17.6 %copy-start.4 = (bf16[2,1024,768]{2,1,0:T(8,128)(2,1)S(1)}, bf16[2,1024,768]{2,1,0:T(8,128)(2,1)}, u32[]{:S(2)}) copy-start(bf16[2,1024,768]{2,1,0:T(8,128)(2,1)} %gather_fusion.19) | copy-start | bytes 9437188
  613.4 34.2 %copy-start.2 = (bf16[2,2048,768]{2,1,0:T(8,128)(2,1)S(1)}, bf16[2,2048,768]{2,1,0:T(8,128)(2,1)}, u32[]{:S(2)}) copy-start(bf16[2,2048,768]{2,1,0:T(8,128)(2,1)} %get-tuple-element.62) | copy-start | bytes 18874372
  647.6 39.6 %copy-start.20 = (f32[2,4096]{1,0:T(2,128)S(1)}, f32[2,4096]{1,0:T(2,128)}, u32[]{:S(2)}) copy-start(f32[2,4096]{1,0:T(2,128)} %multiply_bitcast_fusion.1) | copy-start | bytes 98308
  734.9 1.6 copy-start.14
  735.0 258.5 %all-gather.5.cloned.1.call-start = ((), (), s32[]{:S(2)}) async-start(), calls=%async_computation.4 | async-start | bytes 18874368 | tf_op jit(solution)/shard_map/all_gather | solution.py:38
  741.3 171.3 %copy-start.1 = (s32[16]{0:T(128)S(1)}, s32[16]{0:T(128)}, u32[]{:S(2)}) copy-start(s32[16]{0:T(128)} %copy-done) | copy-start | bytes 196
  741.3 171.3 %copy-start.22 = (s32[2]{0:T(128)S(1)}, s32[2]{0:T(128)}, u32[]{:S(2)}) copy-start(s32[2]{0:T(128)} %copy-done.21) | copy-start | bytes 28
  741.3 171.3 %copy-start.24 = (s32[2]{0:T(128)S(1)}, s32[2]{0:T(128)}, u32[]{:S(2)}) copy-start(s32[2]{0:T(128)} %get-tuple-element.65) | copy-start | bytes 28
  741.3 172.3 %copy-start.16 = (f32[4096,8]{0,1:T(8,128)S(1)}, f32[4096,8]{0,1:T(8,128)}, u32[]{:S(2)}) copy-start(f32[4096,8]{0,1:T(8,128)} %get-tuple-element.61) | copy-start | bytes 393220
  741.3 172.3 %copy-start.17 = (s32[4096,8]{0,1:T(8,128)S(1)}, s32[4096,8]{0,1:T(8,128)}, u32[]{:S(2)}) copy-start(s32[4096,8]{0,1:T(8,128)} %get-tuple-element.59) | copy-start | bytes 393220
  901.4 126.2 %slice-start.8 = ((s8[6291456]{0:T(1024)(128)(4,1)}), s8[2097152]{0:T(1024)(128)(4,1)S(1)}, s32[]{:S(2)}) async-start(s8[6291456]{0:T(1024)(128)(4,1)} %bitcast.191), calls=%async_computation.15 | async-start | bytes 4194304
  912.6 369.5 %reduce-scatter.5.cloned.1.call-start = ((), (), s32[]{:S(2)}) async-start(), calls=%async_computation.5 | async-start | bytes 37748736 | tf_op jit(solution)/shard_map/reduce_scatter | solution.py:50
  993.5 34.1 %slice-start.9 = ((s8[6291456]{0:T(1024)(128)(4,1)}), s8[4194304]{0:T(1024)(128)(4,1)S(1)}, s32[]{:S(2)}) async-start(s8[6291456]{0:T(1024)(128)(4,1)} %bitcast.191), calls=%async_computation.16 | async-start | bytes 8388608
  1115.0 12.3 slice-start.4
  1115.1 12.3 slice-start.6
  1115.1 12.3 slice-start.5
  1115.1 12.5 slice-start.7
  1127.4 6.6 slice-start
  1127.4 7.8 slice-start.2
  1127.6 8.1 slice-start.1
  1127.6 8.7 slice-start.3
  1127.6 14.5 %slice-start.10 = ((s8[6291456]{0:T(1024)(128)(4,1)}), s8[2097152]{0:T(1024)(128)(4,1)S(1)}, s32[]{:S(2)}) async-start(s8[6291456]{0:T(1024)(128)(4,1)} %bitcast.193), calls=%async_computation.17 | async-start | bytes 4194304
  1133.9 8.1 slice-start.11
  1136.3 5.8 copy-start.15
Sparse Core Ops, SparseCore 0:
  114.4 377.3 all-reduce.2
  493.4 80.9 all-gather.2
  735.1 166.2 reduce-scatter.2
  912.7 80.7 all-gather.4
  1115.2 166.9 reduce-scatter.4
where the time goes:
time: 1310 us; the launch traced here: 1300 us
  waiting for transfers between devices  702 us (54%)
  matrix products  272 us (21%)
  local copies, waits for them, and re-layouts  170 us (13%)
  other arithmetic  93.7 us (7%)
  blocking collectives  46.9 us (4%)
  between operations  14.7 us (1%)
    psum x1, waiting for transfers between devices, body(): arrived = lax.psum(outgoing, 'ep')  324 us
    reduce_scatter x2, waiting for transfers between devices, moe_layer(): lax.psum_scatter(partial_sum, 'ep', scatter_dimension=0, tiled=True)  297 us
    dot_general x2, matrix products, moe_layer(): jnp.einsum('jnf,jfd->jnd', inner_act, expert_w[2], preferred_element_type...  95.5 us
    gather x18, local copies, waits for them, and re-layouts, place_moved(): jnp.take(arrived_arr, pick_idx, axis=0)  81.1 us
    all_gather x2, waiting for transfers between devices, moe_layer(): gathered = lax.all_gather(hidden, 'ep', axis=0, tiled=True)  79.7 us
    dot_general x2, matrix products, moe_layer(): jnp.einsum('nd,jdf->jnf', gathered, expert_w[0], preferred_element_type=j...  79.1 us
    dot_general x2, matrix products, moe_layer(): jnp.einsum('nd,jdf->jnf', gathered, expert_w[1], preferred_element_type=j...  68.3 us
    gather x15, local copies, waits for them, and re-layouts, send_moved(): jnp.take(weight_arr, local_idx, axis=0)  61.4 us
  transfers between devices with their start and end apart: 5, of which 4 were waited for; matrix products, arithmetic and copies ran while one was open for 12% of the time, Pallas kernels for 0%

commit v1 on v0

v1 whole, which is shorter than its diff:
```python
import functools

import jax
import jax.numpy as jnp
from jax import lax
from jax.experimental import pallas as pl
from jax.experimental.pallas import tpu as pltpu
from jax.sharding import PartitionSpec as P

TOKEN_AXES = ('replica', 'ep')
MESH = pl.DeviceIdType.MESH
F32, BF16 = jnp.float32, jnp.bfloat16
CORES = 2
CHUNKS = 8
HALF = CHUNKS // 2
STEPS = 17
LANES = 128
TILE = 256
TILES = 18
LAG = 2
TICKS = TILES + 2 * LAG
RING = 6
PRE = {9: 2, 10: 2, 11: 2, 12: 2, 13: 3, 14: 3, 15: 4, 16: 4}


def moe_kernel(group, inject_ref, coef_ref, tok_ref, wg_ref, wu_ref, wd_ref, sg_ref, su_ref, sd_ref,
               out_ref, pg_ref, pu_ref, pd_ref, arr_ref, far_ref,
               blk, part, rdir, rmrg, xin, wgb, wub, wdb, act, cbuf, ct, colb, pick, land, stage,
               ag_send, ag_recv, fw_send, fw_recv, co_send, co_recv, pw_send, pw_recv,
               di_send, di_recv, xi_send, xi_recv, mg_send, mg_recv, wg_sem, wu_sem, wd_sem, io_sem, out_sem,
               pick_sem, mv_send, mv_recv, arr_sem, far_send, far_recv):
    me = lax.axis_index('ep')
    core = lax.rem(me, CORES)
    chip = me // CORES
    right = lax.rem(me + CORES, group)
    left = lax.rem(me + group - CORES, group)
    mate = me + 1 - 2 * core
    rows_all, width = tok_ref.shape
    ffn = sg_ref.shape[2]
    layers = wg_ref.shape[0]
    slots = wg_ref.shape[1]
    piece = rows_all // CHUNKS
    half_rows = rows_all // 2
    total = layers * STEPS

    def remote(src, dst, send, recv, dev):
        return pltpu.make_async_remote_copy(src_ref=src, dst_ref=dst, send_sem=send, recv_sem=recv,
                                            device_id={'ep': dev}, device_id_type=MESH)

    def rows(c):
        return pl.ds(pl.multiple_of(c * piece, piece), piece)

    def own_copy(side, c):
        late = c // HALF
        return remote(blk.at[0, rows(c)], blk.at[1 + late if side == 0 else 2 - late, rows(c)],
                      ag_send.at[side, c], ag_recv.at[side, c], right if side == 0 else left)

    def forward_copy(side, c):
        at = rows(c + side * HALF)
        return remote(blk.at[1, at], blk.at[3, at], fw_send.at[side, c], fw_recv.at[side, c],
                      right if side == 0 else left)

    def coef_copy(n):
        src, dst, dev = ((0, 1, right), (0, 2, left), (1, 3, right))[n]
        return remote(cbuf.at[src], cbuf.at[dst], co_send.at[n], co_recv.at[n], dev)

    def direct_copy(side, c):
        return remote(part.at[1, rows(c + side * HALF)], rdir.at[side, rows(c)], di_send.at[side, c],
                      di_recv.at[side, c], left if side == 0 else right)

    def relay_copy(side, c):
        return remote(part.at[3, rows(c + side * HALF)], xin.at[side, rows(c)], xi_send.at[side, c],
                      xi_recv.at[side, c], right if side == 0 else left)

    def merged_copy(side, c):
        return remote(part.at[2, rows(c + side * HALF)], rmrg.at[side, rows(c)], mg_send.at[side, c],
                      mg_recv.at[side, c], right if side == 0 else left)

    def mate_copies(l, j):
        return [remote(src.at[l, j], dst.at[l, j], pw_send.at[l, j, n], pw_recv.at[l, j, n], mate)
                for n, (src, dst) in enumerate(((wg_ref, pg_ref), (wu_ref, pu_ref), (wd_ref, pd_ref)))]

    def step_kind(i):
        late = i - 5
        turn = late // 4
        unit = jnp.where(i < 5, 0, jnp.where(turn == 0, 1, 4 - turn))
        pos = jnp.where(i < 5, jnp.where(i < 2, i, jnp.where(i == 2, 4, i - 1)), late - 4 * turn)
        kind = jnp.where(pos == 4, 2, jnp.where(pos < 2, 0, 1))
        return unit, kind, jnp.where(pos == 4, 0, lax.rem(pos, 2))

    def fetch(n, which):
        l = n // STEPS
        i = n - l * STEPS
        _, kind, slot = step_kind(i)
        buf = lax.rem(n, 2)

        def go(g, u, d):
            if which == 0:
                pltpu.make_async_copy(g, wgb.at[buf], wg_sem.at[buf]).start()
                pltpu.make_async_copy(u, wub.at[buf], wu_sem.at[buf]).start()
            else:
                pltpu.make_async_copy(d, wdb, wd_sem).start()

        @pl.when(kind == 0)
        def _():
            go(wg_ref.at[l, slot], wu_ref.at[l, slot], wd_ref.at[l, slot])

        @pl.when(kind == 1)
        def _():
            go(pg_ref.at[l, slot], pu_ref.at[l, slot], pd_ref.at[l, slot])

        @pl.when(kind == 2)
        def _():
            go(sg_ref.at[l], su_ref.at[l], sd_ref.at[l])

    def columns(u, first, second):
        mine = jnp.concatenate([cbuf[first, chip][:, :half_rows], cbuf[second, chip][:, half_rows:]], axis=1)
        full = jnp.concatenate([mine, jnp.zeros((LANES - mine.shape[0], rows_all), F32)], axis=0)
        ct[u] = full.T

    def picks(l, t, side):
        quarter = 2 * core + side
        at = lax.rem(t, 6)

        def pair(own, other, r, c):
            spot = (pl.ds(pl.multiple_of(r, TILE), TILE), pl.ds(pl.multiple_of(c, TILE), TILE))
            return (pltpu.make_async_copy(own.at[(l, slice(None)) + spot], pick.at[side, pl.ds(0, slots)], pick_sem.at[side, 0]),
                    pltpu.make_async_copy(other.at[(l, slice(None)) + spot], pick.at[side, pl.ds(slots, slots)], pick_sem.at[side, 1]))

        tall = 2 * TILE * quarter
        r3, c3 = at // 3, lax.rem(at, 3)
        r2, c2 = at // 2, lax.rem(at, 2)
        return (pair(wg_ref, pg_ref, tall + TILE * r3, TILE * c3), pair(wu_ref, pu_ref, tall + TILE * r3, TILE * c3),
                pair(wd_ref, pd_ref, TILE * r2, tall + TILE * c2))

    def pick_start(l, t):
        for side in range(2):
            for n, pair in enumerate(picks(l, t, side)):
                @pl.when(t // 6 == n)
                def _():
                    for copy in pair:
                        copy.start()

    def tile_copy(tick, side):
        return remote(stage.at[lax.rem(tick, 2), side], land.at[side, lax.rem(tick, RING)], mv_send.at[lax.rem(tick, 2), side],
                      mv_recv.at[side, lax.rem(tick, RING)], right if side == 0 else left)

    def tile_store(l, tick, side):
        return pltpu.make_async_copy(land.at[side, lax.rem(tick, RING)], arr_ref.at[l, side, tick], arr_sem.at[side, lax.rem(tick, 2)])

    def ring_step(l, tick):
        inject = inject_ref[l]
        from_here = inject >= 0
        place = jnp.maximum(inject, 0)

        @pl.when(tick < TILES)
        def _():
            for side in range(2):
                for copy in picks(l, tick, side)[0]:
                    copy.wait()

        for side in range(2):
            @pl.when(tick >= 2)
            def _():
                tile_copy(tick - 2, side).wait_send()

            @pl.when(tick >= LAG)
            def _():
                tile_copy(tick - LAG, side).wait_recv()
                tile_store(l, tick - LAG, side).start()
                stage[lax.rem(tick, 2), side] = jnp.where(from_here, pick[side, place], land[side, lax.rem(tick + RING - LAG, RING)])

            @pl.when(tick < LAG)
            def _():
                stage[lax.rem(tick, 2), side] = pick[side, place]

        @pl.when(tick + 1 < TILES)
        def _():
            pick_start(l, tick + 1)

        for side in range(2):
            @pl.when(tick > LAG)
            def _():
                tile_store(l, tick - LAG - 1, side).wait()

            tile_copy(tick, side).start()

    def ring_finish(l):
        for side in range(2):
            tile_store(l, jnp.int32(TICKS - LAG - 1), side).wait()
            for tick in range(TICKS - LAG, TICKS):
                tile_copy(jnp.int32(tick), side).wait_recv()
                tile_store(l, jnp.int32(tick), side).start()
            for tick in range(TICKS - LAG, TICKS):
                tile_store(l, jnp.int32(tick), side).wait()
                tile_copy(jnp.int32(tick), side).wait_send()
        far_copy(l).start()

    def far_copy(l):
        return remote(arr_ref.at[l], far_ref.at[l], far_send.at[l], far_recv.at[l], mate)

    barrier = pltpu.get_barrier_semaphore()
    for dev in (left, right, mate):
        pl.semaphore_signal(barrier, inc=1, device_id={'ep': dev}, device_id_type=MESH)
    pl.semaphore_wait(barrier, 3)

    tok_in = pltpu.make_async_copy(tok_ref, blk.at[0], io_sem.at[0])
    coef_in = pltpu.make_async_copy(coef_ref, cbuf.at[0], io_sem.at[1])
    tok_in.start()
    coef_in.start()
    fetch(jnp.int32(0), 0)
    fetch(jnp.int32(0), 1)
    tok_in.wait()
    for c in range(CHUNKS):
        own_copy(0, c).start()
        own_copy(1, (c + HALF) % CHUNKS).start()
    coef_in.wait()
    coef_copy(0).start()
    coef_copy(1).start()
    for l in range(layers):
        for j in range(slots):
            for copy in mate_copies(l, j):
                copy.start()
    columns(0, 0, 0)

    @pl.loop(0, layers)
    def layer(l):
        @pl.loop(0, STEPS)
        def step(i):
            n = l * STEPS + i
            unit, kind, slot = step_kind(i)
            buf = lax.rem(n, 2)

            for j, at in ((0, 2), (1, 3)):
                @pl.when(i == at)
                def _():
                    for copy in mate_copies(l, j):
                        copy.wait_recv()

            @pl.when(i == 4)
            def _():
                for c in range(HALF):
                    own_copy(0, c).wait_recv()
                    forward_copy(0, c).start()
                    own_copy(1, c + HALF).wait_recv()
                    forward_copy(1, c).start()
                pick_start(l, jnp.int32(0))

                @pl.when(l == 0)
                def _():
                    coef_copy(0).wait_recv()
                    coef_copy(2).start()
                    coef_copy(1).wait_recv()
                    columns(1, 1, 2)
                    columns(2, 2, 1)

            @pl.when(i == 9)
            def _():
                for c in range(HALF):
                    for side in range(2):
                        forward_copy(side, c).wait()

                @pl.when(l == 0)
                def _():
                    coef_copy(2).wait_recv()
                    columns(3, 3, 3)

            @pl.when(i == 13)
            def _():
                for c in range(HALF):
                    own_copy(0, c + HALF).wait_recv()
                    own_copy(1, c).wait_recv()

            for c in range(HALF):
                @pl.when(i == 9 + c)
                def _():
                    direct_copy(0, c).start()
                    direct_copy(1, c).start()

                @pl.when(i == 13 + c)
                def _():
                    relay_copy(0, c).start()
                    relay_copy(1, c).start()

            first, last = jnp.int32(0), jnp.int32(0)
            done = 0
            for at, count in sorted(PRE.items()):
                first = jnp.where(i == at, done, first)
                last = jnp.where(i == at, min(done + count, TICKS), last)
                done = min(done + count, TICKS)
            assert done == TICKS

            @pl.loop(first, last)
            def _(tick):
                ring_step(l, tick)

            pltpu.make_async_copy(wg_ref.at[0, 0], wgb.at[buf], wg_sem.at[buf]).wait()
            pltpu.make_async_copy(wu_ref.at[0, 0], wub.at[buf], wu_sem.at[buf]).wait()

            @pl.when(n + 1 < total)
            def _():
                fetch(n + 1, 0)

            place = 4 * l + jnp.where(kind == 0, 2 * core, 2 * (1 - core)) + slot
            lane = lax.broadcasted_iota(jnp.int32, (rows_all, LANES), 1)
            col = jnp.sum(jnp.where(lane == place, ct[unit], 0.0), axis=1, keepdims=True)
            col = jnp.where(kind == 2, 1.0, col)
            colb[...] = jnp.broadcast_to(col, (rows_all, LANES))

            @pl.when(i == 0)
            def _():
                part[0] = blk[0].astype(F32)

            @pl.when((i == 5) | (i == 9) | (i == 13))
            def _():
                part[unit] = jnp.zeros((rows_all, width), F32)

            @pl.loop(0, ffn // 256)
            def _(f):
                cols = pl.ds(pl.multiple_of(f * 256, 256), 256)
                gate = jnp.dot(blk[unit], wgb[buf, :, cols], preferred_element_type=F32)
                up = jnp.dot(blk[unit], wub[buf, :, cols], preferred_element_type=F32)
                act[:, cols] = (gate / (1.0 + jnp.exp(-gate)) * up).astype(BF16)

            pltpu.make_async_copy(wd_ref.at[0, 0], wdb, wd_sem).wait()

            @pl.loop(0, width // 512)
            def _(w):
                cols = pl.ds(pl.multiple_of(w * 512, 512), 512)
                down = jnp.dot(act[...], wdb[:, cols], preferred_element_type=F32)
                scale = jnp.concatenate([colb[...]] * 4, axis=1)
                part[unit, :, cols] = part[unit, :, cols] + scale * down

            @pl.when(n + 1 < total)
            def _():
                fetch(n + 1, 1)

        for c in range(CHUNKS):
            own_copy(0, c).wait_send()
            own_copy(1, c).wait_send()

        @pl.loop(0, HALF)
        def merge(c):
            for side in range(2):
                relay_copy(side, c).wait_recv()
                at = rows(c + side * HALF)
                part[2, at] = part[2, at] + xin[side, rows(c)]
            for side in range(2):
                merged_copy(side, c).start()

        ring_finish(l)

        @pl.loop(0, HALF)
        def finish(c):
            for side in range(2):
                direct_copy(side, c).wait_recv()
                merged_copy(side, c).wait_recv()
                d = c + side * HALF
                blk[0, rows(d)] = (part[0, rows(d)] + rdir[side, rows(c)] + rmrg[side, rows(c)]).astype(BF16)

            for side in range(2):
                d = c + side * HALF

                @pl.when(l + 1 < layers)
                def _():
                    own_copy(side, d).start()

                @pl.when(l + 1 == layers)
                def _():
                    pltpu.make_async_copy(blk.at[0, rows(d)], out_ref.at[rows(d)], out_sem.at[side, c]).start()

            for side in range(2):
                @pl.when(l + 1 < layers)
                def _():
                    own_copy(1 - side, c + side * HALF).start()

        for c in range(HALF):
            for side in range(2):
                direct_copy(side, c).wait_send()
                relay_copy(side, c).wait_send()
                merged_copy(side, c).wait_send()

    for c in range(HALF):
        for side in range(2):
            d = c + side * HALF
            pltpu.make_async_copy(blk.at[0, rows(d)], out_ref.at[rows(d)], out_sem.at[side, c]).wait()
    for n in range(3):
        coef_copy(n).wait_send()
    for l in range(layers):
        far_copy(l).wait()
        for j in range(slots):
            for copy in mate_copies(l, j):
                copy.wait_send()


def run_moe(group, inject, coef, tok, w_gate, w_up, w_down, sh_gate, sh_up, sh_down):
    n_rows, width = tok.shape
    layers, slots, _, ffn = w_gate.shape
    half = n_rows // 2
    chips = group // CORES
    any_spec = pl.BlockSpec(memory_space=pl.ANY)
    dma = pltpu.SemaphoreType.DMA
    flops = 2 * n_rows * 3 * width * ffn * layers * STEPS
    arrivals = jax.ShapeDtypeStruct((layers, 2, TICKS, TILE, TILE), BF16)
    return pl.pallas_call(
        functools.partial(moe_kernel, group),
        name='moe',
        out_shape=(jax.ShapeDtypeStruct(tok.shape, BF16),) + tuple(
            jax.ShapeDtypeStruct(w.shape, BF16) for w in (w_gate, w_up, w_down)) + (arrivals, arrivals),
        in_specs=[pl.BlockSpec(memory_space=pltpu.SMEM)] + [any_spec] * 8,
        out_specs=[any_spec] * 6,
        scratch_shapes=[
            pltpu.VMEM((chips, n_rows, width), BF16),
            pltpu.VMEM((chips, n_rows, width), F32),
            pltpu.VMEM((2, half, width), F32),
            pltpu.VMEM((2, half, width), F32),
            pltpu.VMEM((2, half, width), F32),
            pltpu.VMEM((2, width, ffn), BF16),
            pltpu.VMEM((2, width, ffn), BF16),
            pltpu.VMEM((ffn, width), BF16),
            pltpu.VMEM((n_rows, ffn), BF16),
            pltpu.VMEM((chips,) + coef.shape, F32),
            pltpu.VMEM((chips, n_rows, LANES), F32),
            pltpu.VMEM((n_rows, LANES), F32),
            pltpu.VMEM((2, CORES * slots, TILE, TILE), BF16),
            pltpu.VMEM((2, RING, TILE, TILE), BF16),
            pltpu.VMEM((2, 2, TILE, TILE), BF16),
            dma((2, CHUNKS)), dma((2, CHUNKS)), dma((2, HALF)), dma((2, HALF)), dma((3,)), dma((3,)),
            dma((layers, slots, 3)), dma((layers, slots, 3)),
            dma((2, HALF)), dma((2, HALF)), dma((2, HALF)), dma((2, HALF)), dma((2, HALF)), dma((2, HALF)),
            dma((2,)), dma((2,)), dma, dma((2,)), dma((2, HALF)),
            dma((2, 2)), dma((2, 2)), dma((2, RING)), dma((2, 2)), dma((layers,)), dma((layers,)),
        ],
        compiler_params=pltpu.CompilerParams(collective_id=0, has_side_effects=True, vmem_limit_bytes=67043328),
        cost_estimate=pl.CostEstimate(flops=flops, bytes_accessed=400 * 2 ** 20, transcendentals=0),
    )(inject, coef, tok, w_gate, w_up, w_down, sh_gate, sh_up, sh_down)


KEEP, NEAR, RINGED = 0, 1, 2
DEPTH = 4


def place_kernel(table_ref, core_ref, wg_ref, wu_ref, wd_ref, pg_ref, pu_ref, pd_ref, arr_ref, far_ref,
                 ng_ref, nu_ref, nd_ref, tall, wide, in_sem, out_sem):
    layers, slots = wg_ref.shape[:2]
    core = core_ref[0]
    jobs = [(l, j, n) for l in range(layers) for j in range(slots) for n in range(3)]

    def parts(k):
        l, j, n = jobs[k]
        own = (wg_ref, wu_ref, wd_ref)[n]
        other = (pg_ref, pu_ref, pd_ref)[n]
        new = (ng_ref, nu_ref, nd_ref)[n]
        buf = (wide if n == 2 else tall).at[k % DEPTH]
        return l, j, n, own, other, new, buf

    def load(k):
        l, j, n, own, other, new, buf = parts(k)
        mode, pos = table_ref[l, j, 0], table_ref[l, j, 1]
        sem = in_sem.at[k % DEPTH]

        @pl.when(mode == KEEP)
        def _():
            pltpu.make_async_copy(own.at[l, j], buf, sem).start()

        @pl.when((mode == NEAR) & (pos < slots))
        def _():
            pltpu.make_async_copy(own.at[l, pos], buf, sem).start()

        @pl.when((mode == NEAR) & (pos >= slots))
        def _():
            pltpu.make_async_copy(other.at[l, pos - slots], buf, sem).start()

        @pl.when(mode == RINGED)
        def _():
            for side in range(2):
                start = table_ref[l, j, 2 + side] + 6 * n
                for source, owner in ((arr_ref, core), (far_ref, 1 - core)):
                    tall_at = 2 * TILE * (2 * owner + side)

                    @pl.loop(0, 6)
                    def _(t):
                        if n == 2:
                            r, c = TILE * (t // 2), tall_at + TILE * lax.rem(t, 2)
                        else:
                            r, c = tall_at + TILE * (t // 3), TILE * lax.rem(t, 3)
                        spot = (pl.ds(pl.multiple_of(r, TILE), TILE), pl.ds(pl.multiple_of(c, TILE), TILE))
                        pltpu.make_async_copy(source.at[l, side, start + t], buf.at[spot], sem).start()

    def arrive(k):
        l, j, n, own, other, new, buf = parts(k)
        pltpu.make_async_copy(own.at[l, j], buf, in_sem.at[k % DEPTH]).wait()

    def store(k):
        l, j, n, own, other, new, buf = parts(k)
        return pltpu.make_async_copy(buf, new.at[l, j], out_sem.at[k % DEPTH])

    ahead = DEPTH - 1
    for k in range(ahead):
        load(k)
    for k in range(len(jobs)):
        arrive(k)
        store(k).start()
        if k >= 1:
            store(k - 1).wait()
        if k + ahead < len(jobs):
            load(k + ahead)
    store(len(jobs) - 1).wait()


def run_place(table, core, w_gate, w_up, w_down, p_gate, p_up, p_down, arrived, far):
    _, _, width, ffn = w_gate.shape
    any_spec = pl.BlockSpec(memory_space=pl.ANY)
    smem = pl.BlockSpec(memory_space=pltpu.SMEM)
    dma = pltpu.SemaphoreType.DMA
    return pl.pallas_call(
        place_kernel,
        name='place',
        out_shape=tuple(jax.ShapeDtypeStruct(w.shape, BF16) for w in (w_gate, w_up, w_down)),
        in_specs=[smem, smem] + [any_spec] * 8,
        out_specs=[any_spec] * 3,
        scratch_shapes=[pltpu.VMEM((DEPTH, width, ffn), BF16), pltpu.VMEM((DEPTH, ffn, width), BF16), dma((DEPTH,)), dma((DEPTH,))],
        compiler_params=pltpu.CompilerParams(vmem_limit_bytes=48 * 2 ** 20),
    )(table, core, w_gate, w_up, w_down, p_gate, p_up, p_down, arrived, far)


def coefficients(routes, gate_vals, old_map, chips):
    layers, n_rows, _ = routes.shape
    n_slots = old_map.shape[1]
    ids = jnp.arange(n_slots, dtype=jnp.int32)
    earlier = (old_map[:, :, None] == old_map[:, None, :]) & (ids[None, :] < ids[:, None])[None]
    serve = jnp.where(jnp.any(earlier, axis=2), 0.0, 1.0)
    hit = routes[:, :, :, None] == old_map[:, None, None, :]
    coef = jnp.sum(jnp.where(hit, gate_vals[..., None], 0.0), axis=2) * serve[:, None, :]
    coef = coef.transpose(2, 0, 1).reshape(chips, n_slots // chips, layers, n_rows)
    return coef.transpose(0, 2, 1, 3).reshape(chips, layers * (n_slots // chips), n_rows)


def plan(old_map, move_slot, move_expert, chips, me, slots):
    layers, n_slots = old_map.shape
    per_chip = n_slots // chips
    chip, core = me // CORES, me % CORES
    holds = (old_map[:, None, :] == move_expert[:, :, None]).reshape(layers, 2, chips, per_chip)
    on_chip = jnp.any(holds, axis=3)
    spot = jnp.argmax(holds, axis=3).astype(jnp.int32)
    first = jnp.argmax(on_chip, axis=2).astype(jnp.int32)
    target = move_slot // per_chip

    def has(m, x):
        return jnp.take_along_axis(on_chip[:, m], x[:, None], axis=1)[:, 0]

    b0, b1 = target[:, 0], target[:, 1]
    near0, near1 = has(0, b0), has(1, b1)
    swap = has(0, b1) & has(1, b0)
    neither = ~near0 & ~near1
    a0 = jnp.where(near0, b0, jnp.where(neither & swap, b1, first[:, 0]))
    a1 = jnp.where(near1, b1, jnp.where(neither & swap, b0, first[:, 1]))
    left_over = neither & ~swap

    def position(index):
        return jnp.where(index // slots == core, index % slots, slots + index % slots)

    source = jnp.stack([a0, a1], axis=1)
    active = (source != target) & jnp.stack([jnp.ones_like(left_over), ~left_over], axis=1)
    here = jnp.where(active & (source == chip), position(spot[:, :, chip]), -1)
    inject = jnp.max(here, axis=1)

    mine = me * slots + jnp.arange(slots, dtype=jnp.int32)
    hit = move_slot[:, None, :] == mine[None, :, None]
    near = jnp.stack([near0, near1], axis=1)
    kind = jnp.where(near, NEAR, jnp.where(active, RINGED, KEEP))
    pos = position(spot[:, :, chip])
    ahead = (target - source) % chips
    fields = jnp.stack([kind, pos, (ahead - 1) * LAG, (chips - ahead - 1) * LAG], axis=2)
    table = jnp.sum(jnp.where(hit[..., None], fields[:, None], 0), axis=2)
    return inject.astype(jnp.int32), table.astype(jnp.int32), left_over


def finish_moves(news, weights, left_over, old_map, move_slot, move_expert, me, slots):
    layers, n_slots = old_map.shape
    ids = jnp.arange(n_slots, dtype=jnp.int32)
    source = jnp.min(jnp.where(old_map == move_expert[:, 1:], ids[None, :], n_slots), axis=1)
    order = jnp.argsort(~left_over)

    def one(k, news):
        l = order[k]
        here = source[l] // slots == me
        there = move_slot[l, 1] // slots == me
        index = move_slot[l, 1] % slots
        out = []
        for new, w in zip(news, weights):
            sent = jnp.where(here, w[l, source[l] % slots], jnp.zeros((), w.dtype))
            got = lax.psum(sent, 'ep')
            out.append(new.at[l, index].set(jnp.where(there, got, new[l, index])))
        return tuple(out)

    return lax.fori_loop(0, jnp.sum(left_over.astype(jnp.int32)), one, news)


def solution(mesh):
    group = mesh.shape['ep']

    def body(tok_in, routes, gate_vals, w_gate, w_up, w_down, sh_gate, sh_up, sh_down, old_map, move_slot, move_expert):
        me = lax.axis_index('ep')
        slots = w_gate.shape[1]
        chips = group // CORES
        coef = coefficients(routes, gate_vals, old_map, chips)
        inject, table, left_over = plan(old_map, move_slot, move_expert, chips, me, slots)
        hidden, p_gate, p_up, p_down, arrived, far = run_moe(group, inject, coef, tok_in, w_gate, w_up, w_down, sh_gate, sh_up, sh_down)
        core = (me % CORES).astype(jnp.int32).reshape(1)
        news = run_place(table, core, w_gate, w_up, w_down, p_gate, p_up, p_down, arrived, far)
        news = finish_moves(news, (w_gate, w_up, w_down), left_over, old_map, move_slot, move_expert, me, slots)
        return (hidden,) + tuple(news)

    weight_spec = P(None, TOKEN_AXES, None, None)
    route_spec = P(None, TOKEN_AXES, None)
    map_spec = P(None, 'replica')
    shared_spec = P(None, None, None)
    tok_spec = P(TOKEN_AXES, None)
    return jax.shard_map(body, mesh=mesh, in_specs=(tok_spec, route_spec, route_spec, weight_spec, weight_spec, weight_spec, shared_spec, shared_spec, shared_spec, map_spec, map_spec, map_spec), out_specs=(tok_spec, weight_spec, weight_spec, weight_spec), check_vma=False)
```

time: 1310 us -> 624 us (0.48)
  waiting for transfers between devices: 702 us -> 0 us
  Pallas kernels: 0 us -> 588 us
  matrix products: 272 us -> 0 us
  local copies, waits for them, and re-layouts: 170 us -> 9.96 us
  other arithmetic: 93.7 us -> 10.6 us
  blocking collectives: 46.9 us -> 0 us
    pallas_call x0 -> x2, Pallas kernels: none -> 588 us  [the longest x1 561 us: run_moe(): pl.pallas_call(functools.partial(moe_kernel, group), name='moe', out_shap...]
    psum x1 -> x0, waiting for transfers between devices: 324 us -> none  [body(): arrived = lax.psum(outgoing, 'ep')]
    reduce_scatter x2 -> x0, waiting for transfers between devices: 297 us -> none  [moe_layer(): lax.psum_scatter(partial_sum, 'ep', scatter_dimension=0, tiled=True)]
    dot_general x10 -> x0, matrix products: 272 us -> none  [the longest x2 95.5 us: moe_layer(): jnp.einsum('jnf,jfd->jnd', inner_act, expert_w[2], preferred_element_type...]
    gather x33 -> x4, local copies, waits for them, and re-layouts: 143 us -> 2.57 us  [has(): return jnp.take_along_axis(on_chip[:, m], x[:, None], axis=1)[:, 0]]
    all_gather x2 -> x0, waiting for transfers between devices: 79.7 us -> none  [moe_layer(): gathered = lax.all_gather(hidden, 'ep', axis=0, tiled=True)]
    select_n x9 -> x4, other arithmetic: 66 us -> 0.69 us  [the longest x1 0.66 us: position(): jnp.where(index // slots == core, index % slots, slots + index % slots)]
    all_gather x2 -> x0, blocking collectives: 46.9 us -> none  [the longest x1 24.9 us: body(): gate_all = lax.all_gather(gate_vals, 'ep', axis=1, tiled=True)]
  transfers between devices with their start and end apart: 5 -> 0, of which waited for: 4 -> 0; matrix products, arithmetic and copies ran while one was open for 12% -> 0% of each run, Pallas kernels for 0% -> 0%
where the time goes in v1:
time: 624 us; the launch traced here: 623 us
  Pallas kernels  588 us (94%)
  between operations  14.2 us (2%)
  other arithmetic  10.6 us (2%)
  local copies, waits for them, and re-layouts  9.96 us (2%)
    pallas_call x1, Pallas kernels, run_moe(): pl.pallas_call(functools.partial(moe_kernel, group), name='moe', out_shap...  561 us
    pallas_call x1, Pallas kernels, run_place(): pl.pallas_call(place_kernel, name='place', out_shape=tuple((jax.ShapeDtyp...  26.6 us

profile of v1, /device:TPU:112, one launch (start us, length us, event | category | flops | bytes accessed | tf_op | source)
XLA Modules:
  0.0 623.0 jit_solution(9341813684003185082)
XLA Ops:
  7.2 0.8 eq.122
  8.0 1.5 compare_reduce_fusion
  9.5 0.7 compare_select_fusion
  10.2 0.1 copy.129
  10.3 0.8 copy.98
  11.1 0.9 compare_reduce_fusion.1
  12.0 0.6 gather_fusion.1
  12.7 0.6 gather_fusion.2
  13.3 0.6 gather_fusion.3
  14.0 0.6 gather_fusion
  14.6 0.7 convert_reduce_fusion
  15.3 0.6 copy_reduce_fusion
  16.0 0.0 copy-start.7
  16.0 1.1 fusion.8
  17.1 0.0 copy-done.7
  17.1 0.9 select_reduce_fusion
  18.0 0.9 and_reduce_fusion.1
  18.9 0.1 bitcast_multiply_fusion
  19.0 0.1 copy.119
  19.1 0.7 reshape.212.coef_ref
  19.8 561.0 %moe.1 = (bf16[512,2048]{1,0:T(8,128)(2,1)}, bf16[2,2,2048,768]{3,2,1,0:T(8,128)(2,1)}, bf16[2,2,2048,768]{3,2,1,0:T(8,128)(2,1)}, bf16[2,2,768,2048]{3,2,1,0:T(...) custom-call(s32[2]{0:T(128)} %get-tuple-element.302.inject_ref, ...), custom_call_target="tpu_custom_call" | custom-call | flops 164282499072 | bytes 419430400 | tf_op jit(solution)/shard_map/moe/pallas_call | solution.py:405
  580.8 0.6 multiply_bitcast_fusion
  581.4 0.1 copy.126
  581.5 0.8 copy.124
  582.3 0.8 copy.125
  583.0 0.8 pad_add_fusion
  583.8 0.8 broadcast_compare_fusion
  584.6 0.1 select_reduce_fusion.1.table_ref
  584.7 0.0 copy-start.8
  584.7 0.0 copy-start.6
  584.7 0.0 copy-start.3
  584.7 0.0 copy-start.4
  584.7 0.0 copy-start.5
  584.7 26.6 %place.1 = (bf16[2,2,2048,768]{3,2,1,0:T(8,128)(2,1)}, bf16[2,2,2048,768]{3,2,1,0:T(8,128)(2,1)}, bf16[2,2,768,2048]{3,2,1,0:T(8,128)(2,1)}) custom-call(s32[2,2,4]{2,1,0:T(2,128)S(1)} %select_reduce_fusion.1.table_ref, s32[1]{0:T(128)} %bitcast.32.core_ref, bf16[2,2,2048,768]{3,2,1,0:T(8,128)(2,1)} %wg_ref.3, bf16[2,2,2048,768]{3,2,1,0:T(8,128)(2,1)} %wu_ref.3, ...), custom_call_target="tpu_custom_call" | custom-call | tf_op jit(solution)/shard_map/place/pallas_call | solution.py:516
  611.3 0.0 copy-done.8
  611.3 0.6 sort.17
  611.9 0.0 copy-done.6
  611.9 0.2 slice_reduce_fusion
  612.1 0.0 copy-done.3
  612.1 0.2 fusion.7
  612.3 0.0 copy-done.4
  612.3 0.0 copy-done.5
  612.3 0.7 while.20
  613.0 3.2 copy.160
  (14 shorter events, 0.1 us)
Async XLA Ops:
  16.0 1.1 copy-start.7
  584.7 26.7 %copy-start.8 = (pred[2,1]{0,1:T(4,128)(4,1)S(1)}, pred[2,1]{0,1:T(4,128)(4,1)}, u32[]{:S(2)}) copy-start(pred[2,1]{0,1:T(4,128)(4,1)} %copy-done.7) | copy-start | bytes 10
  584.7 27.3 %copy-start.6 = (s32[2,2]{1,0:T(2,128)S(1)}, s32[2,2]{1,0:T(2,128)}, u32[]{:S(2)}) copy-start(s32[2,2]{1,0:T(2,128)} %param.33) | copy-start | bytes 52
  584.7 27.5 %copy-start.3 = (s32[2,16]{1,0:T(2,128)S(1)}, s32[2,16]{1,0:T(2,128)}, u32[]{:S(2)}) copy-start(s32[2,16]{1,0:T(2,128)} %param.31) | copy-start | bytes 388
  584.7 27.6 %copy-start.4 = (s32[4]{0:T(128)S(1)}, s32[4]{0:T(128)}, u32[]{:S(2)}) copy-start(s32[4]{0:T(128)} %constant.261.clone.1) | copy-start | bytes 52
  584.7 27.6 %copy-start.5 = (s32[2,2]{1,0:T(2,128)S(1)}, s32[2,2]{1,0:T(2,128)}, u32[]{:S(2)}) copy-start(s32[2,2]{1,0:T(2,128)} %param.32) | copy-start | bytes 52

commit v2 on v1

--- a/solution.py
+++ b/solution.py
@@ -23,9 +23,54 @@
 PRE = {9: 2, 10: 2, 11: 2, 12: 2, 13: 3, 14: 3, 15: 4, 16: 4}
 
 
-def moe_kernel(group, inject_ref, coef_ref, tok_ref, wg_ref, wu_ref, wd_ref, sg_ref, su_ref, sd_ref,
+def read_plan(map_ref, slot_ref, expert_ref, l, chips, per_chip, chip, core, slots):
+    def place_on(m, x):
+        found = per_chip
+        for a in reversed(range(per_chip)):
+            found = jnp.where(map_ref[l, x * per_chip + a] == expert_ref[l, m], a, found)
+        return found
+
+    spots = [[place_on(m, x) for x in range(chips)] for m in range(2)]
+    held = [[s < per_chip for s in row] for row in spots]
+    goals = []
+    for m in range(2):
+        to = slot_ref[l, m]
+        goal = 0
+        for x in range(1, chips):
+            goal = jnp.where(to >= x * per_chip, x, goal)
+        goals.append(goal)
+
+    def has(m, x):
+        out = held[m][0] & (x == 0)
+        for c in range(1, chips):
+            out = out | (held[m][c] & (x == c))
+        return out
+
+    def lowest(m):
+        out = chips - 1
+        for c in reversed(range(chips - 1)):
+            out = jnp.where(held[m][c], c, out)
+        return out
+
+    near = [has(m, goals[m]) for m in range(2)]
+    neither = jnp.logical_not(near[0] | near[1])
+    swap = neither & has(0, goals[1]) & has(1, goals[0])
+    left_over = neither & jnp.logical_not(swap)
+    origin = [jnp.where(near[m], goals[m], jnp.where(swap, goals[1 - m], lowest(m))) for m in range(2)]
+    ringed = [jnp.logical_not(near[0]), jnp.logical_not(near[1] | left_over)]
+    places = []
+    for m in range(2):
+        a = jnp.int32(0)
+        for x in range(chips):
+            a = jnp.where(chip == x, spots[m][x], a)
+        mine = (a >= core * slots) & (a < (core + 1) * slots)
+        places.append(jnp.where(mine, a - core * slots, slots + a - (1 - core) * slots))
+    return goals, origin, near, ringed, left_over, places
+
+
+def moe_kernel(group, map_ref, slot_ref, expert_ref, route_ref, gate_ref, tok_ref, wg_ref, wu_ref, wd_ref, sg_ref, su_ref, sd_ref,
                out_ref, pg_ref, pu_ref, pd_ref, arr_ref, far_ref,
-               blk, part, rdir, rmrg, xin, wgb, wub, wdb, act, cbuf, ct, colb, pick, land, stage,
+               blk, part, rdir, rmrg, xin, wgb, wub, wdb, act, rbuf, gbuf, cbuf, ct, colb, pick, land, stage,
                ag_send, ag_recv, fw_send, fw_recv, co_send, co_recv, pw_send, pw_recv,
                di_send, di_recv, xi_send, xi_recv, mg_send, mg_recv, wg_sem, wu_sem, wd_sem, io_sem, out_sem,
                pick_sem, mv_send, mv_recv, arr_sem, far_send, far_recv):
@@ -42,6 +87,8 @@
     piece = rows_all // CHUNKS
     half_rows = rows_all // 2
     total = layers * STEPS
+    chips = group // CORES
+    n_slots = group * slots
 
     def remote(src, dst, send, recv, dev):
         return pltpu.make_async_remote_copy(src_ref=src, dst_ref=dst, send_sem=send, recv_sem=recv,
@@ -149,9 +196,10 @@
         return pltpu.make_async_copy(land.at[side, lax.rem(tick, RING)], arr_ref.at[l, side, tick], arr_sem.at[side, lax.rem(tick, 2)])
 
     def ring_step(l, tick):
-        inject = inject_ref[l]
-        from_here = inject >= 0
-        place = jnp.maximum(inject, 0)
+        _, origin, _, ringed, _, places = read_plan(map_ref, slot_ref, expert_ref, l, chips, CORES * slots, chip, core, slots)
+        sends = [ringed[m] & (origin[m] == chip) for m in range(2)]
+        from_here = sends[0] | sends[1]
+        place = jnp.where(sends[0], places[0], jnp.where(sends[1], places[1], 0))
 
         @pl.when(tick < TILES)
         def _():
@@ -199,28 +247,42 @@
     def far_copy(l):
         return remote(arr_ref.at[l], far_ref.at[l], far_send.at[l], far_recv.at[l], mate)
 
+    tok_in = pltpu.make_async_copy(tok_ref, blk.at[0], io_sem.at[0])
+    route_in = pltpu.make_async_copy(route_ref, rbuf, io_sem.at[1])
+    gate_in = pltpu.make_async_copy(gate_ref, gbuf, io_sem.at[2])
+    tok_in.start()
+    route_in.start()
+    gate_in.start()
+    fetch(jnp.int32(0), 0)
+    fetch(jnp.int32(0), 1)
+
     barrier = pltpu.get_barrier_semaphore()
     for dev in (left, right, mate):
         pl.semaphore_signal(barrier, inc=1, device_id={'ep': dev}, device_id_type=MESH)
     pl.semaphore_wait(barrier, 3)
 
-    tok_in = pltpu.make_async_copy(tok_ref, blk.at[0], io_sem.at[0])
-    coef_in = pltpu.make_async_copy(coef_ref, cbuf.at[0], io_sem.at[1])
-    tok_in.start()
-    coef_in.start()
-    fetch(jnp.int32(0), 0)
-    fetch(jnp.int32(0), 1)
     tok_in.wait()
     for c in range(CHUNKS):
         own_copy(0, c).start()
         own_copy(1, (c + HALF) % CHUNKS).start()
-    coef_in.wait()
-    coef_copy(0).start()
-    coef_copy(1).start()
     for l in range(layers):
         for j in range(slots):
             for copy in mate_copies(l, j):
                 copy.start()
+
+    route_in.wait()
+    gate_in.wait()
+    for l in range(layers):
+        for q in range(n_slots):
+            expert = map_ref[l, q]
+            serves = jnp.float32(1.0)
+            for p in range(q):
+                serves = jnp.where(map_ref[l, p] == expert, 0.0, serves)
+            gates = jnp.sum(jnp.where(rbuf[l] == expert, gbuf[l], 0.0), axis=0, keepdims=True)
+            at = slots * CORES * l + q % (slots * CORES)
+            cbuf[0, q // (slots * CORES), at:at + 1, :] = gates * serves
+    coef_copy(0).start()
+    coef_copy(1).start()
     columns(0, 0, 0)
 
     @pl.loop(0, layers)
@@ -393,7 +455,7 @@
                 copy.wait_send()
 
 
-def run_moe(group, inject, coef, tok, w_gate, w_up, w_down, sh_gate, sh_up, sh_down):
+def run_moe(group, old_map, move_slot, move_expert, routes, gates, tok, w_gate, w_up, w_down, sh_gate, sh_up, sh_down):
     n_rows, width = tok.shape
     layers, slots, _, ffn = w_gate.shape
     half = n_rows // 2
@@ -407,7 +469,7 @@
         name='moe',
         out_shape=(jax.ShapeDtypeStruct(tok.shape, BF16),) + tuple(
             jax.ShapeDtypeStruct(w.shape, BF16) for w in (w_gate, w_up, w_down)) + (arrivals, arrivals),
-        in_specs=[pl.BlockSpec(memory_space=pltpu.SMEM)] + [any_spec] * 8,
+        in_specs=[pl.BlockSpec(memory_space=pltpu.SMEM)] * 3 + [any_spec] * 9,
         out_specs=[any_spec] * 6,
         scratch_shapes=[
             pltpu.VMEM((chips, n_rows, width), BF16),
@@ -419,7 +481,9 @@
             pltpu.VMEM((2, width, ffn), BF16),
             pltpu.VMEM((ffn, width), BF16),
             pltpu.VMEM((n_rows, ffn), BF16),
-            pltpu.VMEM((chips,) + coef.shape, F32),
+            pltpu.VMEM(routes.shape, jnp.int32),
+            pltpu.VMEM(gates.shape, F32),
+            pltpu.VMEM((chips, chips, layers * slots * CORES, n_rows), F32),
             pltpu.VMEM((chips, n_rows, LANES), F32),
             pltpu.VMEM((n_rows, LANES), F32),
             pltpu.VMEM((2, CORES * slots, TILE, TILE), BF16),
@@ -428,22 +492,39 @@
             dma((2, CHUNKS)), dma((2, CHUNKS)), dma((2, HALF)), dma((2, HALF)), dma((3,)), dma((3,)),
             dma((layers, slots, 3)), dma((layers, slots, 3)),
             dma((2, HALF)), dma((2, HALF)), dma((2, HALF)), dma((2, HALF)), dma((2, HALF)), dma((2, HALF)),
-            dma((2,)), dma((2,)), dma, dma((2,)), dma((2, HALF)),
+            dma((2,)), dma((2,)), dma, dma((3,)), dma((2, HALF)),
             dma((2, 2)), dma((2, 2)), dma((2, RING)), dma((2, 2)), dma((layers,)), dma((layers,)),
         ],
         compiler_params=pltpu.CompilerParams(collective_id=0, has_side_effects=True, vmem_limit_bytes=67043328),
         cost_estimate=pl.CostEstimate(flops=flops, bytes_accessed=400 * 2 ** 20, transcendentals=0),
-    )(inject, coef, tok, w_gate, w_up, w_down, sh_gate, sh_up, sh_down)
+    )(old_map, move_slot, move_expert, routes, gates, tok, w_gate, w_up, w_down, sh_gate, sh_up, sh_down)
 
 
 KEEP, NEAR, RINGED = 0, 1, 2
 DEPTH = 4
 
 
-def place_kernel(table_ref, core_ref, wg_ref, wu_ref, wd_ref, pg_ref, pu_ref, pd_ref, arr_ref, far_ref,
-                 ng_ref, nu_ref, nd_ref, tall, wide, in_sem, out_sem):
+def place_kernel(group, map_ref, slot_ref, expert_ref, wg_ref, wu_ref, wd_ref, pg_ref, pu_ref, pd_ref, arr_ref, far_ref,
+                 ng_ref, nu_ref, nd_ref, over_ref, tall, wide, in_sem, out_sem):
     layers, slots = wg_ref.shape[:2]
-    core = core_ref[0]
+    me = lax.axis_index('ep')
+    core = lax.rem(me, CORES)
+    chip = me // CORES
+    chips = group // CORES
+    table = {}
+    for l in range(layers):
+        goals, origin, near, ringed, left_over, places = read_plan(map_ref, slot_ref, expert_ref, l, chips, CORES * slots, chip, core, slots)
+        over_ref[l] = left_over.astype(jnp.int32)
+        for j in range(slots):
+            mode, pos, first, second = KEEP, 0, 0, 0
+            for m in range(2):
+                here = slot_ref[l, m] == me * slots + j
+                ahead = lax.rem(goals[m] - origin[m] + chips, chips)
+                mode = jnp.where(here, jnp.where(near[m], NEAR, jnp.where(ringed[m], RINGED, KEEP)), mode)
+                pos = jnp.where(here, places[m], pos)
+                first = jnp.where(here, (ahead - 1) * LAG, first)
+                second = jnp.where(here, (chips - ahead - 1) * LAG, second)
+            table[l, j] = mode, pos, (first, second)
     jobs = [(l, j, n) for l in range(layers) for j in range(slots) for n in range(3)]
 
     def parts(k):
@@ -456,7 +537,7 @@
 
     def load(k):
         l, j, n, own, other, new, buf = parts(k)
-        mode, pos = table_ref[l, j, 0], table_ref[l, j, 1]
+        mode, pos, starts = table[l, j]
         sem = in_sem.at[k % DEPTH]
 
         @pl.when(mode == KEEP)
@@ -474,7 +555,7 @@
         @pl.when(mode == RINGED)
         def _():
             for side in range(2):
-                start = table_ref[l, j, 2 + side] + 6 * n
+                start = starts[side] + 6 * n
                 for source, owner in ((arr_ref, core), (far_ref, 1 - core)):
                     tall_at = 2 * TILE * (2 * owner + side)
 
@@ -508,108 +589,56 @@
     store(len(jobs) - 1).wait()
 
 
-def run_place(table, core, w_gate, w_up, w_down, p_gate, p_up, p_down, arrived, far):
-    _, _, width, ffn = w_gate.shape
+def run_place(group, old_map, move_slot, move_expert, w_gate, w_up, w_down, p_gate, p_up, p_down, arrived, far):
+    layers, _, width, ffn = w_gate.shape
     any_spec = pl.BlockSpec(memory_space=pl.ANY)
     smem = pl.BlockSpec(memory_space=pltpu.SMEM)
     dma = pltpu.SemaphoreType.DMA
     return pl.pallas_call(
-        place_kernel,
+        functools.partial(place_kernel, group),
         name='place',
-        out_shape=tuple(jax.ShapeDtypeStruct(w.shape, BF16) for w in (w_gate, w_up, w_down)),
-        in_specs=[smem, smem] + [any_spec] * 8,
-        out_specs=[any_spec] * 3,
+        out_shape=tuple(jax.ShapeDtypeStruct(w.shape, BF16) for w in (w_gate, w_up, w_down)) + (
+            jax.ShapeDtypeStruct((layers,), jnp.int32),),
+        in_specs=[smem] * 3 + [any_spec] * 8,
+        out_specs=[any_spec] * 3 + [smem],
         scratch_shapes=[pltpu.VMEM((DEPTH, width, ffn), BF16), pltpu.VMEM((DEPTH, ffn, width), BF16), dma((DEPTH,)), dma((DEPTH,))],
         compiler_params=pltpu.CompilerParams(vmem_limit_bytes=48 * 2 ** 20),
-    )(table, core, w_gate, w_up, w_down, p_gate, p_up, p_down, arrived, far)
-
-
-def coefficients(routes, gate_vals, old_map, chips):
-    layers, n_rows, _ = routes.shape
-    n_slots = old_map.shape[1]
-    ids = jnp.arange(n_slots, dtype=jnp.int32)
-    earlier = (old_map[:, :, None] == old_map[:, None, :]) & (ids[None, :] < ids[:, None])[None]
-    serve = jnp.where(jnp.any(earlier, axis=2), 0.0, 1.0)
-    hit = routes[:, :, :, None] == old_map[:, None, None, :]
-    coef = jnp.sum(jnp.where(hit, gate_vals[..., None], 0.0), axis=2) * serve[:, None, :]
-    coef = coef.transpose(2, 0, 1).reshape(chips, n_slots // chips, layers, n_rows)
-    return coef.transpose(0, 2, 1, 3).reshape(chips, layers * (n_slots // chips), n_rows)
-
-
-def plan(old_map, move_slot, move_expert, chips, me, slots):
+    )(old_map, move_slot, move_expert, w_gate, w_up, w_down, p_gate, p_up, p_down, arrived, far)
+
+
+def finish_moves(group, news, weights, over, old_map, move_slot, move_expert):
     layers, n_slots = old_map.shape
-    per_chip = n_slots // chips
-    chip, core = me // CORES, me % CORES
-    holds = (old_map[:, None, :] == move_expert[:, :, None]).reshape(layers, 2, chips, per_chip)
-    on_chip = jnp.any(holds, axis=3)
-    spot = jnp.argmax(holds, axis=3).astype(jnp.int32)
-    first = jnp.argmax(on_chip, axis=2).astype(jnp.int32)
-    target = move_slot // per_chip
-
-    def has(m, x):
-        return jnp.take_along_axis(on_chip[:, m], x[:, None], axis=1)[:, 0]
-
-    b0, b1 = target[:, 0], target[:, 1]
-    near0, near1 = has(0, b0), has(1, b1)
-    swap = has(0, b1) & has(1, b0)
-    neither = ~near0 & ~near1
-    a0 = jnp.where(near0, b0, jnp.where(neither & swap, b1, first[:, 0]))
-    a1 = jnp.where(near1, b1, jnp.where(neither & swap, b0, first[:, 1]))
-    left_over = neither & ~swap
-
-    def position(index):
-        return jnp.where(index // slots == core, index % slots, slots + index % slots)
-
-    source = jnp.stack([a0, a1], axis=1)
-    active = (source != target) & jnp.stack([jnp.ones_like(left_over), ~left_over], axis=1)
-    here = jnp.where(active & (source == chip), position(spot[:, :, chip]), -1)
-    inject = jnp.max(here, axis=1)
-
-    mine = me * slots + jnp.arange(slots, dtype=jnp.int32)
-    hit = move_slot[:, None, :] == mine[None, :, None]
-    near = jnp.stack([near0, near1], axis=1)
-    kind = jnp.where(near, NEAR, jnp.where(active, RINGED, KEEP))
-    pos = position(spot[:, :, chip])
-    ahead = (target - source) % chips
-    fields = jnp.stack([kind, pos, (ahead - 1) * LAG, (chips - ahead - 1) * LAG], axis=2)
-    table = jnp.sum(jnp.where(hit[..., None], fields[:, None], 0), axis=2)
-    return inject.astype(jnp.int32), table.astype(jnp.int32), left_over
-
-
-def finish_moves(news, weights, left_over, old_map, move_slot, move_expert, me, slots):
-    layers, n_slots = old_map.shape
-    ids = jnp.arange(n_slots, dtype=jnp.int32)
-    source = jnp.min(jnp.where(old_map == move_expert[:, 1:], ids[None, :], n_slots), axis=1)
-    order = jnp.argsort(~left_over)
+    slots = weights[0].shape[1]
+    ring = [(d, (d + 1) % group) for d in range(group)]
 
     def one(k, news):
-        l = order[k]
-        here = source[l] // slots == me
+        me = lax.axis_index('ep')
+        l = jnp.where(over[0] > 0, k, layers - 1)
+        ids = jnp.arange(n_slots, dtype=jnp.int32)
+        source = jnp.min(jnp.where(old_map[l] == move_expert[l, 1], ids, n_slots))
+        here = source // slots == me
         there = move_slot[l, 1] // slots == me
         index = move_slot[l, 1] % slots
-        out = []
-        for new, w in zip(news, weights):
-            sent = jnp.where(here, w[l, source[l] % slots], jnp.zeros((), w.dtype))
-            got = lax.psum(sent, 'ep')
-            out.append(new.at[l, index].set(jnp.where(there, got, new[l, index])))
-        return tuple(out)
-
-    return lax.fori_loop(0, jnp.sum(left_over.astype(jnp.int32)), one, news)
+        own = tuple(w[l, source % slots] for w in weights)
+
+        def hop(_, held):
+            return tuple(jnp.where(here, o, lax.ppermute(h, 'ep', ring)) for o, h in zip(own, held))
+
+        got = lax.fori_loop(0, group - 1, hop, own)
+        return tuple(new.at[l, index].set(jnp.where(there, g, new[l, index])) for new, g in zip(news, got))
+
+    return lax.fori_loop(0, jnp.sum(over), one, news)
 
 
 def solution(mesh):
     group = mesh.shape['ep']
 
     def body(tok_in, routes, gate_vals, w_gate, w_up, w_down, sh_gate, sh_up, sh_down, old_map, move_slot, move_expert):
-        me = lax.axis_index('ep')
-        slots = w_gate.shape[1]
-        chips = group // CORES
-        coef = coefficients(routes, gate_vals, old_map, chips)
-        inject, table, left_over = plan(old_map, move_slot, move_expert, chips, me, slots)
-        hidden, p_gate, p_up, p_down, arrived, far = run_moe(group, inject, coef, tok_in, w_gate, w_up, w_down, sh_gate, sh_up, sh_down)
-        core = (me % CORES).astype(jnp.int32).reshape(1)
-        news = run_place(table, core, w_gate, w_up, w_down, p_gate, p_up, p_down, arrived, far)
-        news = finish_moves(news, (w_gate, w_up, w_down), left_over, old_map, move_slot, move_expert, me, slots)
+        maps = (old_map, move_slot, move_expert)
+        by_choice = (routes.transpose(0, 2, 1), gate_vals.transpose(0, 2, 1))
+        hidden, p_gate, p_up, p_down, arrived, far = run_moe(group, *maps, *by_choice, tok_in, w_gate, w_up, w_down, sh_gate, sh_up, sh_down)
+        *news, over = run_place(group, *maps, w_gate, w_up, w_down, p_gate, p_up, p_down, arrived, far)
+        news = finish_moves(group, tuple(news), (w_gate, w_up, w_down), over, *maps)
         return (hidden,) + tuple(news)
 
     weight_spec = P(None, TOKEN_AXES, None, None)

time: 624 us -> 596 us (0.955)
  between operations: 14.2 us -> 0.73 us
  other arithmetic: 10.6 us -> 0.71 us
  local copies, waits for them, and re-layouts: 9.96 us -> 3.19 us
where the time goes in v2:
time: 596 us
  Pallas kernels  590 us (99%)
    pallas_call x1, Pallas kernels, run_moe(): pl.pallas_call(functools.partial(moe_kernel, group), name='moe', out_shap...  562 us
    pallas_call x1, Pallas kernels, run_place(): pl.pallas_call(functools.partial(place_kernel, group), name='place', out_...  27.8 us

profile of v2, /device:TPU:112, one launch (start us, length us, event | category | flops | bytes accessed | tf_op | source)
XLA Modules:
  0.0 595.6 jit_solution(7173508648238661069)
XLA Ops:
  0.6 562.5 %moe.1 = (bf16[512,2048]{1,0:T(8,128)(2,1)}, bf16[2,2,2048,768]{3,2,1,0:T(8,128)(2,1)}, bf16[2,2,2048,768]{3,2,1,0:T(8,128)(2,1)}, bf16[2,2,768,2048]{3,2,1,0:T(...) custom-call(s32[2,16]{1,0:T(2,128)} %map_ref.3, s32[2,2]{1,0:T(2,128)} %slot_ref.3, ...), custom_call_target="tpu_custom_call" | custom-call | flops 164282499072 | bytes 419430400 | tf_op jit(solution)/shard_map/moe/pallas_call | solution.py:467
  563.1 0.0 copy-start.7
  563.1 0.0 copy-start.8
  563.1 0.0 copy-start.9
  563.1 0.0 copy-start.10
  563.1 27.8 %place.1 = (bf16[2,2,2048,768]{3,2,1,0:T(8,128)(2,1)}, bf16[2,2,2048,768]{3,2,1,0:T(8,128)(2,1)}, bf16[2,2,768,2048]{3,2,1,0:T(8,128)(2,1)}, s32[2]{0:T(128)S(1)}) custom-call(s32[2,16]{1,0:T(2,128)} %map_ref.3, s32[2,2]{1,0:T(2,128)} %slot_ref.3, s32[2,2]{1,0:T(2,128)} %expert_ref.3, bf16[2,2,2048,768]{3,2,1,0:T(8,128)(2,1)} %wg_ref.3, ...), custom_call_target="tpu_custom_call" | custom-call | tf_op jit(solution)/shard_map/place/pallas_call | solution.py:597
  591.0 0.7 reduce_sum.9
  591.7 0.0 copy-done.7
  591.7 0.0 copy-done.8
  591.7 0.0 copy-done.9
  591.7 0.0 copy-done.10
  591.7 0.7 while.53
  592.4 3.2 copy.44
Async XLA Ops:
  563.1 28.6 %copy-start.7 = (s32[4]{0:T(128)S(1)}, s32[4]{0:T(128)}, u32[]{:S(2)}) copy-start(s32[4]{0:T(128)} %constant.175.clone.1) | copy-start | bytes 52
  563.1 28.6 %copy-start.8 = (s32[2,16]{1,0:T(2,128)S(1)}, s32[2,16]{1,0:T(2,128)}, u32[]{:S(2)}) copy-start(s32[2,16]{1,0:T(2,128)} %map_ref.3) | copy-start | bytes 388
  563.1 28.6 %copy-start.9 = (s32[2,2]{1,0:T(2,128)S(1)}, s32[2,2]{1,0:T(2,128)}, u32[]{:S(2)}) copy-start(s32[2,2]{1,0:T(2,128)} %slot_ref.3) | copy-start | bytes 52
  563.1 28.6 %copy-start.10 = (s32[2,2]{1,0:T(2,128)S(1)}, s32[2,2]{1,0:T(2,128)}, u32[]{:S(2)}) copy-start(s32[2,2]{1,0:T(2,128)} %expert_ref.3) | copy-start | bytes 52

commit v3 on v2

--- a/solution.py
+++ b/solution.py
@@ -69,10 +69,10 @@
 
 
 def moe_kernel(group, map_ref, slot_ref, expert_ref, route_ref, gate_ref, tok_ref, wg_ref, wu_ref, wd_ref, sg_ref, su_ref, sd_ref,
-               out_ref, pg_ref, pu_ref, pd_ref, arr_ref, far_ref,
+               base_ref, first_ref, second_ref, pg_ref, pu_ref, pd_ref, arr_ref, far_ref,
                blk, part, rdir, rmrg, xin, wgb, wub, wdb, act, rbuf, gbuf, cbuf, ct, colb, pick, land, stage,
                ag_send, ag_recv, fw_send, fw_recv, co_send, co_recv, pw_send, pw_recv,
-               di_send, di_recv, xi_send, xi_recv, mg_send, mg_recv, wg_sem, wu_sem, wd_sem, io_sem, out_sem,
+               di_send, di_recv, xi_send, xi_recv, mg_send, mg_recv, wg_sem, wu_sem, wd_sem, io_sem, out_sem, sum_sem,
                pick_sem, mv_send, mv_recv, arr_sem, far_send, far_recv):
     me = lax.axis_index('ep')
     core = lax.rem(me, CORES)
@@ -123,6 +123,13 @@
         return remote(part.at[2, rows(c + side * HALF)], rmrg.at[side, rows(c)], mg_send.at[side, c],
                       mg_recv.at[side, c], right if side == 0 else left)
 
+    def sum_out(side, c):
+        return pltpu.make_async_copy(part.at[2, rows(c + side * HALF)], (first_ref, second_ref)[side].at[rows(c)], sum_sem.at[side, c])
+
+    def base_out(side, c):
+        d = rows(c + side * HALF)
+        return pltpu.make_async_copy(part.at[0, d], base_ref.at[d], out_sem.at[side, c])
+
     def mate_copies(l, j):
         return [remote(src.at[l, j], dst.at[l, j], pw_send.at[l, j, n], pw_recv.at[l, j, n], mate)
                 for n, (src, dst) in enumerate(((wg_ref, pg_ref), (wu_ref, pu_ref), (wd_ref, pd_ref)))]
@@ -408,44 +415,54 @@
                 at = rows(c + side * HALF)
                 part[2, at] = part[2, at] + xin[side, rows(c)]
             for side in range(2):
-                merged_copy(side, c).start()
+                @pl.when(l + 1 < layers)
+                def _():
+                    merged_copy(side, c).start()
+
+                @pl.when(l + 1 == layers)
+                def _():
+                    sum_out(side, c).start()
 
         ring_finish(l)
 
-        @pl.loop(0, HALF)
-        def finish(c):
-            for side in range(2):
-                direct_copy(side, c).wait_recv()
-                merged_copy(side, c).wait_recv()
-                d = c + side * HALF
-                blk[0, rows(d)] = (part[0, rows(d)] + rdir[side, rows(c)] + rmrg[side, rows(c)]).astype(BF16)
-
-            for side in range(2):
-                d = c + side * HALF
-
-                @pl.when(l + 1 < layers)
-                def _():
-                    own_copy(side, d).start()
-
-                @pl.when(l + 1 == layers)
-                def _():
-                    pltpu.make_async_copy(blk.at[0, rows(d)], out_ref.at[rows(d)], out_sem.at[side, c]).start()
-
-            for side in range(2):
-                @pl.when(l + 1 < layers)
-                def _():
+        @pl.when(l + 1 < layers)
+        def _():
+            @pl.loop(0, HALF)
+            def finish(c):
+                for side in range(2):
+                    direct_copy(side, c).wait_recv()
+                    merged_copy(side, c).wait_recv()
+                    d = c + side * HALF
+                    blk[0, rows(d)] = (part[0, rows(d)] + rdir[side, rows(c)] + rmrg[side, rows(c)]).astype(BF16)
+                for side in range(2):
+                    own_copy(side, c + side * HALF).start()
+                for side in range(2):
                     own_copy(1 - side, c + side * HALF).start()
+
+            for c in range(HALF):
+                for side in range(2):
+                    merged_copy(side, c).wait_send()
+
+        @pl.when(l + 1 == layers)
+        def _():
+            @pl.loop(0, HALF)
+            def finish(c):
+                for side in range(2):
+                    direct_copy(side, c).wait_recv()
+                    d = rows(c + side * HALF)
+                    part[0, d] = part[0, d] + rdir[side, rows(c)]
+                for side in range(2):
+                    base_out(side, c).start()
 
         for c in range(HALF):
             for side in range(2):
                 direct_copy(side, c).wait_send()
                 relay_copy(side, c).wait_send()
-                merged_copy(side, c).wait_send()
 
     for c in range(HALF):
         for side in range(2):
-            d = c + side * HALF
-            pltpu.make_async_copy(blk.at[0, rows(d)], out_ref.at[rows(d)], out_sem.at[side, c]).wait()
+            sum_out(side, c).wait()
+            base_out(side, c).wait()
     for n in range(3):
         coef_copy(n).wait_send()
     for l in range(layers):
@@ -467,10 +484,10 @@
     return pl.pallas_call(
         functools.partial(moe_kernel, group),
         name='moe',
-        out_shape=(jax.ShapeDtypeStruct(tok.shape, BF16),) + tuple(
+        out_shape=(jax.ShapeDtypeStruct(tok.shape, F32),) + (jax.ShapeDtypeStruct((half, width), F32),) * 2 + tuple(
             jax.ShapeDtypeStruct(w.shape, BF16) for w in (w_gate, w_up, w_down)) + (arrivals, arrivals),
         in_specs=[pl.BlockSpec(memory_space=pltpu.SMEM)] * 3 + [any_spec] * 9,
-        out_specs=[any_spec] * 6,
+        out_specs=[any_spec] * 8,
         scratch_shapes=[
             pltpu.VMEM((chips, n_rows, width), BF16),
             pltpu.VMEM((chips, n_rows, width), F32),
@@ -492,7 +509,7 @@
             dma((2, CHUNKS)), dma((2, CHUNKS)), dma((2, HALF)), dma((2, HALF)), dma((3,)), dma((3,)),
             dma((layers, slots, 3)), dma((layers, slots, 3)),
             dma((2, HALF)), dma((2, HALF)), dma((2, HALF)), dma((2, HALF)), dma((2, HALF)), dma((2, HALF)),
-            dma((2,)), dma((2,)), dma, dma((3,)), dma((2, HALF)),
+            dma((2,)), dma((2,)), dma, dma((3,)), dma((2, HALF)), dma((2, HALF)),
             dma((2, 2)), dma((2, 2)), dma((2, RING)), dma((2, 2)), dma((layers,)), dma((layers,)),
         ],
         compiler_params=pltpu.CompilerParams(collective_id=0, has_side_effects=True, vmem_limit_bytes=67043328),
@@ -603,6 +620,7 @@
         out_specs=[any_spec] * 3 + [smem],
         scratch_shapes=[pltpu.VMEM((DEPTH, width, ffn), BF16), pltpu.VMEM((DEPTH, ffn, width), BF16), dma((DEPTH,)), dma((DEPTH,))],
         compiler_params=pltpu.CompilerParams(vmem_limit_bytes=48 * 2 ** 20),
+        cost_estimate=pl.CostEstimate(flops=2 * 10 ** 10, bytes_accessed=80 * 10 ** 6, transcendentals=0),
     )(old_map, move_slot, move_expert, w_gate, w_up, w_down, p_gate, p_up, p_down, arrived, far)
 
 
@@ -636,9 +654,12 @@
     def body(tok_in, routes, gate_vals, w_gate, w_up, w_down, sh_gate, sh_up, sh_down, old_map, move_slot, move_expert):
         maps = (old_map, move_slot, move_expert)
         by_choice = (routes.transpose(0, 2, 1), gate_vals.transpose(0, 2, 1))
-        hidden, p_gate, p_up, p_down, arrived, far = run_moe(group, *maps, *by_choice, tok_in, w_gate, w_up, w_down, sh_gate, sh_up, sh_down)
+        base, first, second, p_gate, p_up, p_down, arrived, far = run_moe(group, *maps, *by_choice, tok_in, w_gate, w_up, w_down, sh_gate, sh_up, sh_down)
         *news, over = run_place(group, *maps, w_gate, w_up, w_down, p_gate, p_up, p_down, arrived, far)
         news = finish_moves(group, tuple(news), (w_gate, w_up, w_down), over, *maps)
+        rightward = [(d, (d + CORES) % group) for d in range(group)]
+        leftward = [(d, (d + group - CORES) % group) for d in range(group)]
+        hidden = (base + jnp.concatenate([lax.ppermute(first, 'ep', rightward), lax.ppermute(second, 'ep', leftward)], axis=0)).astype(BF16)
         return (hidden,) + tuple(news)
 
     weight_spec = P(None, TOKEN_AXES, None, None)

time: 596 us -> 588 us (0.987)
  Pallas kernels: 590 us -> 560 us
  waiting for transfers between devices: 0 us -> 17.6 us
    pallas_call x1, Pallas kernels: 562 us -> 532 us  [run_moe(): pl.pallas_call(functools.partial(moe_kernel, group), name='moe', out_shap...]
    ppermute x0 -> x2, waiting for transfers between devices: none -> 17.6 us  [the longest x1 17.6 us: body(): lax.ppermute(first, 'ep', rightward)]
  transfers between devices with their start and end apart: 0 -> 2, of which waited for: 0 -> 1; matrix products, arithmetic and copies ran while one was open for 0% -> 0% of each run, Pallas kernels for 0% -> 5%
where the time goes in v3:
time: 588 us
  Pallas kernels  560 us (95%)
  waiting for transfers between devices  17.6 us (3%)
    pallas_call x1, Pallas kernels, run_moe(): pl.pallas_call(functools.partial(moe_kernel, group), name='moe', out_shap...  532 us
    pallas_call x1, Pallas kernels, run_place(): pl.pallas_call(functools.partial(place_kernel, group), name='place', out_...  27.5 us
    ppermute x1, waiting for transfers between devices, body(): lax.ppermute(first, 'ep', rightward)  17.6 us
  transfers between devices with their start and end apart: 2, of which 1 were waited for; matrix products, arithmetic and copies ran while one was open for 0% of the time, Pallas kernels for 5%

profile of v3, /device:TPU:112, one launch (start us, length us, event | category | flops | bytes accessed | tf_op | source)
XLA Modules:
  0.0 587.6 jit_solution(15957925476052642230)
XLA Ops:
  0.6 532.0 %moe.1 = (f32[512,2048]{1,0:T(8,128)}, f32[256,2048]{1,0:T(8,128)}, f32[256,2048]{1,0:T(8,128)}, bf16[2,2,2048,768]{3,2,1,0:T(8,128)(2,1)}, bf16[2,2,2048,768]{3...) custom-call(s32[2,16]{1,0:T(2,128)} %map_ref.3, ...), custom_call_target="tpu_custom_call" | custom-call | flops 164282499072 | bytes 419430400 | tf_op jit(solution)/shard_map/moe/pallas_call | solution.py:484
  532.7 0.9 collective-permute-start.3
  533.6 2.4 collective-permute-start.4
  536.0 27.5 %place.1 = (bf16[2,2,2048,768]{3,2,1,0:T(8,128)(2,1)}, bf16[2,2,2048,768]{3,2,1,0:T(8,128)(2,1)}, bf16[2,2,768,2048]{3,2,1,0:T(8,128)(2,1)}, s32[2]{0:T(128)S(1)}) custom-call(s32[2,16]{1,0:T(2,128)} %map_ref.3, s32[2,2]{1,0:T(2,128)} %slot_ref.3, s32[2,2]{1,0:T(2,128)} %expert_ref.3, bf16[2,2,2048,768]{3,2,1,0:T(8,128)(2,1)} %wg_ref.3, ...), custom_call_target="tpu_custom_call" | custom-call | flops 20000000000 | bytes 80000000 | tf_op jit(solution)/shard_map/place/pallas_call | solution.py:614
  563.5 0.6 reduce_sum.9
  564.2 17.6 %collective-permute-done.3 = f32[256,2048]{1,0:T(8,128)S(1)} collective-permute-done((f32[256,2048]{1,0:T(8,128)}, f32[256,2048]{1,0:T(8,128)S(1)}, u32[]{:S(2)}, u32[]{:S(2)}) %collective-permute-start.3) | collective-permute-done | bytes 2097184 | tf_op jit(solution)/shard_map/ppermute | solution.py:662
  581.8 0.0 collective-permute-done.4
  581.8 0.0 copy-start.7
  581.8 0.0 copy-start.8
  581.8 0.0 copy-start.9
  581.8 0.0 copy-start.10
  581.8 4.9 fusion.4
  586.7 0.0 copy-done.7
  586.7 0.0 copy-done.8
  586.7 0.0 copy-done.9
  586.7 0.0 copy-done.10
  586.7 0.7 while.53
Async XLA Ops:
  532.7 49.1 %collective-permute-start.3 = (f32[256,2048]{1,0:T(8,128)}, f32[256,2048]{1,0:T(8,128)S(1)}, u32[]{:S(2)}, u32[]{:S(2)}) collective-permute-start(f32[256,2048]{1,0:T(8,128)} %get-tuple-element.316), channel_id=1, source_target_pairs={{0,2},{1,3},{2,4},{3,5},{4,6},{5,7},{6,0},{7,1},{8,10},{9,11},{10,... | collective-permute-start | bytes 6291464 | tf_op jit(solution)/shard_map/ppermute | solution.py:662
  533.6 48.2 %collective-permute-start.4 = (f32[256,2048]{1,0:T(8,128)}, f32[256,2048]{1,0:T(8,128)}, u32[]{:S(2)}, u32[]{:S(2)}) collective-permute-start(f32[256,2048]{1,0:T(8,128)} %get-tuple-element.317), channel_id=1, source_target_pairs={{0,6},{1,7},{2,0},{3,1},{4,2},{5,3},{6,4},{7,5},{8,14},{9,15},{10,... | collective-permute-start | bytes 6291464 | tf_op jit(solution)/shard_map/ppermute | solution.py:662
  581.8 4.9 copy-start.7
  581.8 4.9 copy-start.8
  581.8 4.9 copy-start.9
  581.8 4.9 copy-start.10

commit v4 on v3

--- a/solution.py
+++ b/solution.py
@@ -199,8 +199,17 @@
         return remote(stage.at[lax.rem(tick, 2), side], land.at[side, lax.rem(tick, RING)], mv_send.at[lax.rem(tick, 2), side],
                       mv_recv.at[side, lax.rem(tick, RING)], right if side == 0 else left)
 
-    def tile_store(l, tick, side):
-        return pltpu.make_async_copy(land.at[side, lax.rem(tick, RING)], arr_ref.at[l, side, tick], arr_sem.at[side, lax.rem(tick, 2)])
+    def tile_out(l, tick, side, begin):
+        tile = land.at[side, lax.rem(tick, RING)]
+        turn = lax.rem(tick, 2)
+        keep = pltpu.make_async_copy(tile, arr_ref.at[l, side, tick], arr_sem.at[side, turn])
+        give = remote(tile, far_ref.at[l, side, tick], far_send.at[side, turn], far_recv.at[l], mate)
+        if begin:
+            keep.start()
+            give.start()
+        else:
+            keep.wait()
+            give.wait_send()
 
     def ring_step(l, tick):
         _, origin, _, ringed, _, places = read_plan(map_ref, slot_ref, expert_ref, l, chips, CORES * slots, chip, core, slots)
@@ -222,7 +231,7 @@
             @pl.when(tick >= LAG)
             def _():
                 tile_copy(tick - LAG, side).wait_recv()
-                tile_store(l, tick - LAG, side).start()
+                tile_out(l, tick - LAG, side, True)
                 stage[lax.rem(tick, 2), side] = jnp.where(from_here, pick[side, place], land[side, lax.rem(tick + RING - LAG, RING)])
 
             @pl.when(tick < LAG)
@@ -236,23 +245,19 @@
         for side in range(2):
             @pl.when(tick > LAG)
             def _():
-                tile_store(l, tick - LAG - 1, side).wait()
+                tile_out(l, tick - LAG - 1, side, False)
 
             tile_copy(tick, side).start()
 
     def ring_finish(l):
         for side in range(2):
-            tile_store(l, jnp.int32(TICKS - LAG - 1), side).wait()
+            tile_out(l, jnp.int32(TICKS - LAG - 1), side, False)
             for tick in range(TICKS - LAG, TICKS):
                 tile_copy(jnp.int32(tick), side).wait_recv()
-                tile_store(l, jnp.int32(tick), side).start()
+                tile_out(l, jnp.int32(tick), side, True)
             for tick in range(TICKS - LAG, TICKS):
-                tile_store(l, jnp.int32(tick), side).wait()
+                tile_out(l, jnp.int32(tick), side, False)
                 tile_copy(jnp.int32(tick), side).wait_send()
-        far_copy(l).start()
-
-    def far_copy(l):
-        return remote(arr_ref.at[l], far_ref.at[l], far_send.at[l], far_recv.at[l], mate)
 
     tok_in = pltpu.make_async_copy(tok_ref, blk.at[0], io_sem.at[0])
     route_in = pltpu.make_async_copy(route_ref, rbuf, io_sem.at[1])
@@ -466,7 +471,7 @@
     for n in range(3):
         coef_copy(n).wait_send()
     for l in range(layers):
-        far_copy(l).wait()
+        pltpu.make_async_copy(arr_ref.at[l], far_ref.at[l], far_recv.at[l]).wait()
         for j in range(slots):
             for copy in mate_copies(l, j):
                 copy.wait_send()
@@ -510,7 +515,7 @@
             dma((layers, slots, 3)), dma((layers, slots, 3)),
             dma((2, HALF)), dma((2, HALF)), dma((2, HALF)), dma((2, HALF)), dma((2, HALF)), dma((2, HALF)),
             dma((2,)), dma((2,)), dma, dma((3,)), dma((2, HALF)), dma((2, HALF)),
-            dma((2, 2)), dma((2, 2)), dma((2, RING)), dma((2, 2)), dma((layers,)), dma((layers,)),
+            dma((2, 2)), dma((2, 2)), dma((2, RING)), dma((2, 2)), dma((2, 2)), dma((layers,)),
         ],
         compiler_params=pltpu.CompilerParams(collective_id=0, has_side_effects=True, vmem_limit_bytes=67043328),
         cost_estimate=pl.CostEstimate(flops=flops, bytes_accessed=400 * 2 ** 20, transcendentals=0),

time: 588 us -> 580 us (0.986)
  Pallas kernels: 560 us -> 553 us
    pallas_call x1, Pallas kernels: 532 us -> 526 us  [run_moe(): pl.pallas_call(functools.partial(moe_kernel, group), name='moe', out_shap...]
where the time goes in v4:
time: 580 us; the launch traced here: 579 us
  Pallas kernels  553 us (95%)
  waiting for transfers between devices  15.4 us (3%)
    pallas_call x1, Pallas kernels, run_moe(): pl.pallas_call(functools.partial(moe_kernel, group), name='moe', out_shap...  526 us
    pallas_call x1, Pallas kernels, run_place(): pl.pallas_call(functools.partial(place_kernel, group), name='place', out_...  27.5 us
    ppermute x1, waiting for transfers between devices, body(): lax.ppermute(first, 'ep', rightward)  15.4 us
  transfers between devices with their start and end apart: 2, of which 1 were waited for; matrix products, arithmetic and copies ran while one was open for 0% of the time, Pallas kernels for 5%

profile of v4, /device:TPU:112, one launch (start us, length us, event | category | flops | bytes accessed | tf_op | source)
XLA Modules:
  0.0 579.1 jit_solution(13839043130933240318)
XLA Ops:
  0.6 525.7 %moe.1 = (f32[512,2048]{1,0:T(8,128)}, f32[256,2048]{1,0:T(8,128)}, f32[256,2048]{1,0:T(8,128)}, bf16[2,2,2048,768]{3,2,1,0:T(8,128)(2,1)}, bf16[2,2,2048,768]{3...) custom-call(s32[2,16]{1,0:T(2,128)} %map_ref.3, ...), custom_call_target="tpu_custom_call" | custom-call | flops 164282499072 | bytes 419430400 | tf_op jit(solution)/shard_map/moe/pallas_call | solution.py:489
  526.3 0.8 collective-permute-start.3
  527.2 2.5 collective-permute-start.4
  529.6 27.5 %place.1 = (bf16[2,2,2048,768]{3,2,1,0:T(8,128)(2,1)}, bf16[2,2,2048,768]{3,2,1,0:T(8,128)(2,1)}, bf16[2,2,768,2048]{3,2,1,0:T(8,128)(2,1)}, s32[2]{0:T(128)S(1)}) custom-call(s32[2,16]{1,0:T(2,128)} %map_ref.3, s32[2,2]{1,0:T(2,128)} %slot_ref.3, s32[2,2]{1,0:T(2,128)} %expert_ref.3, bf16[2,2,2048,768]{3,2,1,0:T(8,128)(2,1)} %wg_ref.3, ...), custom_call_target="tpu_custom_call" | custom-call | flops 20000000000 | bytes 80000000 | tf_op jit(solution)/shard_map/place/pallas_call | solution.py:619
  557.1 0.6 reduce_sum.9
  557.8 15.4 %collective-permute-done.3 = f32[256,2048]{1,0:T(8,128)S(1)} collective-permute-done((f32[256,2048]{1,0:T(8,128)}, f32[256,2048]{1,0:T(8,128)S(1)}, u32[]{:S(2)}, u32[]{:S(2)}) %collective-permute-start.3) | collective-permute-done | bytes 2097184 | tf_op jit(solution)/shard_map/ppermute | solution.py:667
  573.3 0.0 collective-permute-done.4
  573.3 0.0 copy-start.7
  573.3 0.0 copy-start.8
  573.3 0.0 copy-start.9
  573.3 0.0 copy-start.10
  573.3 4.9 fusion.4
  578.1 0.0 copy-done.7
  578.1 0.0 copy-done.8
  578.1 0.0 copy-done.9
  578.2 0.0 copy-done.10
  578.2 0.7 while.53
Async XLA Ops:
  526.3 46.9 %collective-permute-start.3 = (f32[256,2048]{1,0:T(8,128)}, f32[256,2048]{1,0:T(8,128)S(1)}, u32[]{:S(2)}, u32[]{:S(2)}) collective-permute-start(f32[256,2048]{1,0:T(8,128)} %get-tuple-element.316), channel_id=1, source_target_pairs={{0,2},{1,3},{2,4},{3,5},{4,6},{5,7},{6,0},{7,1},{8,10},{9,11},{10,... | collective-permute-start | bytes 6291464 | tf_op jit(solution)/shard_map/ppermute | solution.py:667
  527.2 46.1 %collective-permute-start.4 = (f32[256,2048]{1,0:T(8,128)}, f32[256,2048]{1,0:T(8,128)}, u32[]{:S(2)}, u32[]{:S(2)}) collective-permute-start(f32[256,2048]{1,0:T(8,128)} %get-tuple-element.317), channel_id=1, source_target_pairs={{0,6},{1,7},{2,0},{3,1},{4,2},{5,3},{6,4},{7,5},{8,14},{9,15},{10,... | collective-permute-start | bytes 6291464 | tf_op jit(solution)/shard_map/ppermute | solution.py:667
  573.3 4.9 copy-start.7
  573.3 4.9 copy-start.8
  573.3 4.9 copy-start.9
  573.3 4.9 copy-start.10

commit v5 on v4

--- a/solution.py
+++ b/solution.py
@@ -17,10 +17,11 @@
 LANES = 128
 TILE = 256
 TILES = 18
-LAG = 2
+LAG = 1
 TICKS = TILES + 2 * LAG
-RING = 6
-PRE = {9: 2, 10: 2, 11: 2, 12: 2, 13: 3, 14: 3, 15: 4, 16: 4}
+RING = 4
+PIECES = 8
+FIRST = 5
 
 
 def read_plan(map_ref, slot_ref, expert_ref, l, chips, per_chip, chip, core, slots):
@@ -97,6 +98,10 @@
     def rows(c):
         return pl.ds(pl.multiple_of(c * piece, piece), piece)
 
+    def sums(c):
+        size = half_rows // PIECES
+        return pl.ds(pl.multiple_of(c * size, size), size)
+
     def own_copy(side, c):
         late = c // HALF
         return remote(blk.at[0, rows(c)], blk.at[1 + late if side == 0 else 2 - late, rows(c)],
@@ -112,22 +117,22 @@
         return remote(cbuf.at[src], cbuf.at[dst], co_send.at[n], co_recv.at[n], dev)
 
     def direct_copy(side, c):
-        return remote(part.at[1, rows(c + side * HALF)], rdir.at[side, rows(c)], di_send.at[side, c],
+        return remote(part.at[1, sums(c + side * PIECES)], rdir.at[side, sums(c)], di_send.at[side, c],
                       di_recv.at[side, c], left if side == 0 else right)
 
     def relay_copy(side, c):
-        return remote(part.at[3, rows(c + side * HALF)], xin.at[side, rows(c)], xi_send.at[side, c],
+        return remote(part.at[3, sums(c + side * PIECES)], xin.at[side, sums(c)], xi_send.at[side, c],
                       xi_recv.at[side, c], right if side == 0 else left)
 
     def merged_copy(side, c):
-        return remote(part.at[2, rows(c + side * HALF)], rmrg.at[side, rows(c)], mg_send.at[side, c],
+        return remote(part.at[2, sums(c + side * PIECES)], rmrg.at[side, sums(c)], mg_send.at[side, c],
                       mg_recv.at[side, c], right if side == 0 else left)
 
     def sum_out(side, c):
-        return pltpu.make_async_copy(part.at[2, rows(c + side * HALF)], (first_ref, second_ref)[side].at[rows(c)], sum_sem.at[side, c])
+        return pltpu.make_async_copy(part.at[2, sums(c + side * PIECES)], (first_ref, second_ref)[side].at[sums(c)], sum_sem.at[side, c])
 
     def base_out(side, c):
-        d = rows(c + side * HALF)
+        d = sums(c + side * PIECES)
         return pltpu.make_async_copy(part.at[0, d], base_ref.at[d], out_sem.at[side, c])
 
     def mate_copies(l, j):
@@ -249,6 +254,24 @@
 
             tile_copy(tick, side).start()
 
+    def beat(l, k):
+        ring_step(l, k)
+
+        @pl.when(k < HALF)
+        def _():
+            own_copy(0, k + HALF).start()
+            own_copy(1, k).start()
+
+        @pl.when((k >= HALF) & (k < HALF + PIECES))
+        def _():
+            direct_copy(0, k - HALF).start()
+            direct_copy(1, k - HALF).start()
+
+        @pl.when(k >= HALF + PIECES)
+        def _():
+            relay_copy(0, k - HALF - PIECES).start()
+            relay_copy(1, k - HALF - PIECES).start()
+
     def ring_finish(l):
         for side in range(2):
             tile_out(l, jnp.int32(TICKS - LAG - 1), side, False)
@@ -257,6 +280,7 @@
                 tile_out(l, jnp.int32(tick), side, True)
             for tick in range(TICKS - LAG, TICKS):
                 tile_out(l, jnp.int32(tick), side, False)
+            for tick in range(TICKS - 2, TICKS):
                 tile_copy(jnp.int32(tick), side).wait_send()
 
     tok_in = pltpu.make_async_copy(tok_ref, blk.at[0], io_sem.at[0])
@@ -274,9 +298,9 @@
     pl.semaphore_wait(barrier, 3)
 
     tok_in.wait()
-    for c in range(CHUNKS):
+    for c in range(HALF):
         own_copy(0, c).start()
-        own_copy(1, (c + HALF) % CHUNKS).start()
+        own_copy(1, c + HALF).start()
     for l in range(layers):
         for j in range(slots):
             for copy in mate_copies(l, j):
@@ -311,13 +335,17 @@
                     for copy in mate_copies(l, j):
                         copy.wait_recv()
 
+            for at, pieces in ((2, (0,)), (3, (1, 2)), (4, (3,))):
+                @pl.when(i == at)
+                def _():
+                    for c in pieces:
+                        own_copy(0, c).wait_recv()
+                        forward_copy(0, c).start()
+                        own_copy(1, c + HALF).wait_recv()
+                        forward_copy(1, c).start()
+
             @pl.when(i == 4)
             def _():
-                for c in range(HALF):
-                    own_copy(0, c).wait_recv()
-                    forward_copy(0, c).start()
-                    own_copy(1, c + HALF).wait_recv()
-                    forward_copy(1, c).start()
                 pick_start(l, jnp.int32(0))
 
                 @pl.when(l == 0)
@@ -345,28 +373,11 @@
                     own_copy(0, c + HALF).wait_recv()
                     own_copy(1, c).wait_recv()
 
-            for c in range(HALF):
-                @pl.when(i == 9 + c)
-                def _():
-                    direct_copy(0, c).start()
-                    direct_copy(1, c).start()
-
-                @pl.when(i == 13 + c)
-                def _():
-                    relay_copy(0, c).start()
-                    relay_copy(1, c).start()
-
-            first, last = jnp.int32(0), jnp.int32(0)
-            done = 0
-            for at, count in sorted(PRE.items()):
-                first = jnp.where(i == at, done, first)
-                last = jnp.where(i == at, min(done + count, TICKS), last)
-                done = min(done + count, TICKS)
-            assert done == TICKS
-
-            @pl.loop(first, last)
-            def _(tick):
-                ring_step(l, tick)
+            tick = jnp.where(i < FIRST + HALF, i - FIRST, HALF + 2 * (i - FIRST - HALF))
+
+            @pl.when(i >= FIRST)
+            def _():
+                beat(l, tick)
 
             pltpu.make_async_copy(wg_ref.at[0, 0], wgb.at[buf], wg_sem.at[buf]).wait()
             pltpu.make_async_copy(wu_ref.at[0, 0], wub.at[buf], wu_sem.at[buf]).wait()
@@ -396,6 +407,10 @@
                 up = jnp.dot(blk[unit], wub[buf, :, cols], preferred_element_type=F32)
                 act[:, cols] = (gate / (1.0 + jnp.exp(-gate)) * up).astype(BF16)
 
+            @pl.when(i >= FIRST + HALF)
+            def _():
+                beat(l, tick + 1)
+
             pltpu.make_async_copy(wd_ref.at[0, 0], wdb, wd_sem).wait()
 
             @pl.loop(0, width // 512)
@@ -413,12 +428,12 @@
             own_copy(0, c).wait_send()
             own_copy(1, c).wait_send()
 
-        @pl.loop(0, HALF)
+        @pl.loop(0, PIECES)
         def merge(c):
             for side in range(2):
                 relay_copy(side, c).wait_recv()
-                at = rows(c + side * HALF)
-                part[2, at] = part[2, at] + xin[side, rows(c)]
+                at = sums(c + side * PIECES)
+                part[2, at] = part[2, at] + xin[side, sums(c)]
             for side in range(2):
                 @pl.when(l + 1 < layers)
                 def _():
@@ -435,36 +450,35 @@
             @pl.loop(0, HALF)
             def finish(c):
                 for side in range(2):
-                    direct_copy(side, c).wait_recv()
-                    merged_copy(side, c).wait_recv()
-                    d = c + side * HALF
-                    blk[0, rows(d)] = (part[0, rows(d)] + rdir[side, rows(c)] + rmrg[side, rows(c)]).astype(BF16)
+                    for p in range(PIECES // HALF):
+                        direct_copy(side, c * (PIECES // HALF) + p).wait_recv()
+                        merged_copy(side, c * (PIECES // HALF) + p).wait_recv()
+                    d = rows(c + side * HALF)
+                    blk[0, d] = (part[0, d] + rdir[side, rows(c)] + rmrg[side, rows(c)]).astype(BF16)
                 for side in range(2):
                     own_copy(side, c + side * HALF).start()
-                for side in range(2):
-                    own_copy(1 - side, c + side * HALF).start()
-
-            for c in range(HALF):
+
+            for c in range(PIECES):
                 for side in range(2):
                     merged_copy(side, c).wait_send()
 
         @pl.when(l + 1 == layers)
         def _():
-            @pl.loop(0, HALF)
+            @pl.loop(0, PIECES)
             def finish(c):
                 for side in range(2):
                     direct_copy(side, c).wait_recv()
-                    d = rows(c + side * HALF)
-                    part[0, d] = part[0, d] + rdir[side, rows(c)]
+                    d = sums(c + side * PIECES)
+                    part[0, d] = part[0, d] + rdir[side, sums(c)]
                 for side in range(2):
                     base_out(side, c).start()
 
-        for c in range(HALF):
+        for c in range(PIECES):
             for side in range(2):
                 direct_copy(side, c).wait_send()
                 relay_copy(side, c).wait_send()
 
-    for c in range(HALF):
+    for c in range(PIECES):
         for side in range(2):
             sum_out(side, c).wait()
             base_out(side, c).wait()
@@ -513,8 +527,8 @@
             pltpu.VMEM((2, 2, TILE, TILE), BF16),
             dma((2, CHUNKS)), dma((2, CHUNKS)), dma((2, HALF)), dma((2, HALF)), dma((3,)), dma((3,)),
             dma((layers, slots, 3)), dma((layers, slots, 3)),
-            dma((2, HALF)), dma((2, HALF)), dma((2, HALF)), dma((2, HALF)), dma((2, HALF)), dma((2, HALF)),
-            dma((2,)), dma((2,)), dma, dma((3,)), dma((2, HALF)), dma((2, HALF)),
+            dma((2, PIECES)), dma((2, PIECES)), dma((2, PIECES)), dma((2, PIECES)), dma((2, PIECES)), dma((2, PIECES)),
+            dma((2,)), dma((2,)), dma, dma((3,)), dma((2, PIECES)), dma((2, PIECES)),
             dma((2, 2)), dma((2, 2)), dma((2, RING)), dma((2, 2)), dma((2, 2)), dma((layers,)),
         ],
         compiler_params=pltpu.CompilerParams(collective_id=0, has_side_effects=True, vmem_limit_bytes=67043328),

time: 580 us -> 543 us (0.936)
  Pallas kernels: 553 us -> 515 us
    pallas_call x1, Pallas kernels: 526 us -> 488 us  [run_moe(): pl.pallas_call(functools.partial(moe_kernel, group), name='moe', out_shap...]
where the time goes in v5:
time: 543 us
  Pallas kernels  515 us (95%)
  waiting for transfers between devices  16.7 us (3%)
  other arithmetic  5.49 us (1%)
    pallas_call x1, Pallas kernels, run_moe(): pl.pallas_call(functools.partial(moe_kernel, group), name='moe', out_shap...  488 us
    pallas_call x1, Pallas kernels, run_place(): pl.pallas_call(functools.partial(place_kernel, group), name='place', out_...  27.5 us
    ppermute x1, waiting for transfers between devices, body(): lax.ppermute(first, 'ep', rightward)  16.7 us
  transfers between devices with their start and end apart: 2, of which 1 were waited for; matrix products, arithmetic and copies ran while one was open for 0% of the time, Pallas kernels for 5%

profile of v5, /device:TPU:112, one launch (start us, length us, event | category | flops | bytes accessed | tf_op | source)
XLA Modules:
  0.0 542.5 jit_solution(9455866230065950864)
XLA Ops:
  0.6 487.9 %moe.1 = (f32[512,2048]{1,0:T(8,128)}, f32[256,2048]{1,0:T(8,128)}, f32[256,2048]{1,0:T(8,128)}, bf16[2,2,2048,768]{3,2,1,0:T(8,128)(2,1)}, bf16[2,2,2048,768]{3...) custom-call(s32[2,16]{1,0:T(2,128)} %map_ref.3, ...), custom_call_target="tpu_custom_call" | custom-call | flops 164282499072 | bytes 419430400 | tf_op jit(solution)/shard_map/moe/pallas_call | solution.py:503
  488.5 0.3 collective-permute-start.3
  488.8 3.0 collective-permute-start.4
  491.9 27.5 %place.1 = (bf16[2,2,2048,768]{3,2,1,0:T(8,128)(2,1)}, bf16[2,2,2048,768]{3,2,1,0:T(8,128)(2,1)}, bf16[2,2,768,2048]{3,2,1,0:T(8,128)(2,1)}, s32[2]{0:T(128)S(1)}) custom-call(s32[2,16]{1,0:T(2,128)} %map_ref.3, s32[2,2]{1,0:T(2,128)} %slot_ref.3, s32[2,2]{1,0:T(2,128)} %expert_ref.3, bf16[2,2,2048,768]{3,2,1,0:T(8,128)(2,1)} %wg_ref.3, ...), custom_call_target="tpu_custom_call" | custom-call | flops 20000000000 | bytes 80000000 | tf_op jit(solution)/shard_map/place/pallas_call | solution.py:633
  519.4 0.6 reduce_sum.9
  520.0 16.7 %collective-permute-done.3 = f32[256,2048]{1,0:T(8,128)S(1)} collective-permute-done((f32[256,2048]{1,0:T(8,128)}, f32[256,2048]{1,0:T(8,128)S(1)}, u32[]{:S(2)}, u32[]{:S(2)}) %collective-permute-start.3) | collective-permute-done | bytes 2097184 | tf_op jit(solution)/shard_map/ppermute | solution.py:681
  536.7 0.0 collective-permute-done.4
  536.7 0.0 copy-start.7
  536.7 0.0 copy-start.8
  536.7 0.0 copy-start.9
  536.7 0.0 copy-start.10
  536.7 4.9 fusion.4
  541.6 0.0 copy-done.7
  541.6 0.0 copy-done.8
  541.6 0.0 copy-done.9
  541.6 0.0 copy-done.10
  541.6 0.7 while.53
Async XLA Ops:
  488.5 48.2 %collective-permute-start.3 = (f32[256,2048]{1,0:T(8,128)}, f32[256,2048]{1,0:T(8,128)S(1)}, u32[]{:S(2)}, u32[]{:S(2)}) collective-permute-start(f32[256,2048]{1,0:T(8,128)} %get-tuple-element.316), channel_id=1, source_target_pairs={{0,2},{1,3},{2,4},{3,5},{4,6},{5,7},{6,0},{7,1},{8,10},{9,11},{10,... | collective-permute-start | bytes 6291464 | tf_op jit(solution)/shard_map/ppermute | solution.py:681
  488.8 47.9 %collective-permute-start.4 = (f32[256,2048]{1,0:T(8,128)}, f32[256,2048]{1,0:T(8,128)}, u32[]{:S(2)}, u32[]{:S(2)}) collective-permute-start(f32[256,2048]{1,0:T(8,128)} %get-tuple-element.317), channel_id=1, source_target_pairs={{0,6},{1,7},{2,0},{3,1},{4,2},{5,3},{6,4},{7,5},{8,14},{9,15},{10,... | collective-permute-start | bytes 6291464 | tf_op jit(solution)/shard_map/ppermute | solution.py:681
  536.7 4.9 copy-start.7
  536.7 4.9 copy-start.8
  536.7 4.9 copy-start.9
  536.7 4.9 copy-start.10

commit v6 on v5

--- a/solution.py
+++ b/solution.py
@@ -16,11 +16,12 @@
 STEPS = 17
 LANES = 128
 TILE = 256
-TILES = 18
-LAG = 1
-TICKS = TILES + 2 * LAG
+TILES = 36
+PER = TILES // 3
+TICKS = TILES // 2 + 1
 RING = 4
 PIECES = 8
+EARLY = 5
 FIRST = 5
 
 
@@ -71,8 +72,8 @@
 
 def moe_kernel(group, map_ref, slot_ref, expert_ref, route_ref, gate_ref, tok_ref, wg_ref, wu_ref, wd_ref, sg_ref, su_ref, sd_ref,
                base_ref, first_ref, second_ref, pg_ref, pu_ref, pd_ref, arr_ref, far_ref,
-               blk, part, rdir, rmrg, xin, wgb, wub, wdb, act, rbuf, gbuf, cbuf, ct, colb, pick, land, stage,
-               ag_send, ag_recv, fw_send, fw_recv, co_send, co_recv, pw_send, pw_recv,
+               blk, part, rdir, rmrg, xin, wgb, wub, wdb, act, rbuf, gbuf, cbuf, cgot, ct, colb, pick, land, stage, inject_ref,
+               ag_send, le_recv, la_recv, fw_send, fw_recv, co_send, co_recv, pw_send, pw_recv,
                di_send, di_recv, xi_send, xi_recv, mg_send, mg_recv, wg_sem, wu_sem, wd_sem, io_sem, out_sem, sum_sem,
                pick_sem, mv_send, mv_recv, arr_sem, far_send, far_recv):
     me = lax.axis_index('ep')
@@ -80,6 +81,7 @@
     chip = me // CORES
     right = lax.rem(me + CORES, group)
     left = lax.rem(me + group - CORES, group)
+    across = lax.rem(me + 2 * CORES, group)
     mate = me + 1 - 2 * core
     rows_all, width = tok_ref.shape
     ffn = sg_ref.shape[2]
@@ -102,41 +104,52 @@
         size = half_rows // PIECES
         return pl.ds(pl.multiple_of(c * size, size), size)
 
-    def own_copy(side, c):
-        late = c // HALF
-        return remote(blk.at[0, rows(c)], blk.at[1 + late if side == 0 else 2 - late, rows(c)],
-                      ag_send.at[side, c], ag_recv.at[side, c], right if side == 0 else left)
+    def halves(c, side):
+        return sums(c + side * PIECES)
+
+    def whole_half(side):
+        return pl.ds(side * half_rows, half_rows)
+
+    def lead_copy(side, c):
+        at = rows(c + side * HALF)
+        return remote(blk.at[0, at], blk.at[1, at], ag_send.at[side], le_recv.at[side, c], right if side == 0 else left)
+
+    def late_copy(side, c):
+        at = rows(c + (1 - side) * HALF)
+        return remote(blk.at[0, at], blk.at[2, at], ag_send.at[side], la_recv.at[side], right if side == 0 else left)
 
     def forward_copy(side, c):
         at = rows(c + side * HALF)
-        return remote(blk.at[1, at], blk.at[3, at], fw_send.at[side, c], fw_recv.at[side, c],
-                      right if side == 0 else left)
+        return remote(blk.at[1, at], blk.at[3, at], fw_send.at[side], fw_recv.at[side], right if side == 0 else left)
 
     def coef_copy(n):
-        src, dst, dev = ((0, 1, right), (0, 2, left), (1, 3, right))[n]
-        return remote(cbuf.at[src], cbuf.at[dst], co_send.at[n], co_recv.at[n], dev)
+        ahead, dev = ((1, right), (chips - 1, left), (2, across))[n]
+        return remote(cbuf.at[lax.rem(chip + ahead, chips)], cgot.at[n], co_send, co_recv, dev)
 
     def direct_copy(side, c):
-        return remote(part.at[1, sums(c + side * PIECES)], rdir.at[side, sums(c)], di_send.at[side, c],
-                      di_recv.at[side, c], left if side == 0 else right)
+        return remote(part.at[1, halves(c, side)], rdir.at[side, sums(c)], di_send.at[side], di_recv.at[side],
+                      left if side == 0 else right)
 
     def relay_copy(side, c):
-        return remote(part.at[3, sums(c + side * PIECES)], xin.at[side, sums(c)], xi_send.at[side, c],
-                      xi_recv.at[side, c], right if side == 0 else left)
+        return remote(part.at[3, halves(c, side)], xin.at[side, sums(c)], xi_send.at[side],
+                      xi_recv.at[side, jnp.maximum(c - EARLY, 0)], right if side == 0 else left)
 
     def merged_copy(side, c):
-        return remote(part.at[2, sums(c + side * PIECES)], rmrg.at[side, sums(c)], mg_send.at[side, c],
-                      mg_recv.at[side, c], right if side == 0 else left)
+        return remote(part.at[2, halves(c, side)], rmrg.at[side, sums(c)], mg_send.at[side],
+                      mg_recv.at[side, c // (PIECES // HALF)], right if side == 0 else left)
 
     def sum_out(side, c):
-        return pltpu.make_async_copy(part.at[2, sums(c + side * PIECES)], (first_ref, second_ref)[side].at[sums(c)], sum_sem.at[side, c])
+        return pltpu.make_async_copy(part.at[2, halves(c, side)], (first_ref, second_ref)[side].at[sums(c)], sum_sem.at[side])
 
     def base_out(side, c):
-        d = sums(c + side * PIECES)
-        return pltpu.make_async_copy(part.at[0, d], base_ref.at[d], out_sem.at[side, c])
+        d = halves(c, side)
+        return pltpu.make_async_copy(part.at[0, d], base_ref.at[d], out_sem.at[side])
+
+    def await_bytes(like, sem):
+        pltpu.make_async_copy(like, like, sem).wait()
 
     def mate_copies(l, j):
-        return [remote(src.at[l, j], dst.at[l, j], pw_send.at[l, j, n], pw_recv.at[l, j, n], mate)
+        return [remote(src.at[l, j], dst.at[l, j], pw_send.at[n], pw_recv.at[l, j, n], mate)
                 for n, (src, dst) in enumerate(((wg_ref, pg_ref), (wu_ref, pu_ref), (wd_ref, pd_ref)))]
 
     def step_kind(i):
@@ -173,29 +186,32 @@
             go(sg_ref.at[l], su_ref.at[l], sd_ref.at[l])
 
     def columns(u, first, second):
-        mine = jnp.concatenate([cbuf[first, chip][:, :half_rows], cbuf[second, chip][:, half_rows:]], axis=1)
+        mine = jnp.concatenate([first[:, :half_rows], second[:, half_rows:]], axis=1)
         full = jnp.concatenate([mine, jnp.zeros((LANES - mine.shape[0], rows_all), F32)], axis=0)
         ct[u] = full.T
 
     def picks(l, t, side):
-        quarter = 2 * core + side
-        at = lax.rem(t, 6)
+        tile = t if side == 0 else TILES - 1 - t
+        at = lax.rem(tile, PER)
+        across_ffn, across_half = ffn // TILE, PER // (ffn // TILE)
 
         def pair(own, other, r, c):
             spot = (pl.ds(pl.multiple_of(r, TILE), TILE), pl.ds(pl.multiple_of(c, TILE), TILE))
             return (pltpu.make_async_copy(own.at[(l, slice(None)) + spot], pick.at[side, pl.ds(0, slots)], pick_sem.at[side, 0]),
                     pltpu.make_async_copy(other.at[(l, slice(None)) + spot], pick.at[side, pl.ds(slots, slots)], pick_sem.at[side, 1]))
 
-        tall = 2 * TILE * quarter
-        r3, c3 = at // 3, lax.rem(at, 3)
-        r2, c2 = at // 2, lax.rem(at, 2)
-        return (pair(wg_ref, pg_ref, tall + TILE * r3, TILE * c3), pair(wu_ref, pu_ref, tall + TILE * r3, TILE * c3),
-                pair(wd_ref, pd_ref, TILE * r2, tall + TILE * c2))
+        mine = across_half * TILE * core
+        tall = (mine + TILE * (at // across_ffn), TILE * lax.rem(at, across_ffn))
+        wide = (TILE * (at // across_half), mine + TILE * lax.rem(at, across_half))
+        up = pair(wu_ref, pu_ref, *tall)
+        if side == 0:
+            return (tile < PER, pair(wg_ref, pg_ref, *tall)), (tile >= PER, up)
+        return (tile >= 2 * PER, pair(wd_ref, pd_ref, *wide)), (tile < 2 * PER, up)
 
     def pick_start(l, t):
         for side in range(2):
-            for n, pair in enumerate(picks(l, t, side)):
-                @pl.when(t // 6 == n)
+            for there, pair in picks(l, t, side):
+                @pl.when(there)
                 def _():
                     for copy in pair:
                         copy.start()
@@ -217,50 +233,48 @@
             give.wait_send()
 
     def ring_step(l, tick):
-        _, origin, _, ringed, _, places = read_plan(map_ref, slot_ref, expert_ref, l, chips, CORES * slots, chip, core, slots)
-        sends = [ringed[m] & (origin[m] == chip) for m in range(2)]
-        from_here = sends[0] | sends[1]
-        place = jnp.where(sends[0], places[0], jnp.where(sends[1], places[1], 0))
-
-        @pl.when(tick < TILES)
-        def _():
-            for side in range(2):
-                for copy in picks(l, tick, side)[0]:
-                    copy.wait()
+        inject = inject_ref[l]
+        from_here = inject >= 0
+        place = jnp.maximum(inject, 0)
+        for side in range(2):
+            for copy in picks(l, tick, side)[0][1]:
+                copy.wait()
 
         for side in range(2):
             @pl.when(tick >= 2)
             def _():
                 tile_copy(tick - 2, side).wait_send()
 
-            @pl.when(tick >= LAG)
-            def _():
-                tile_copy(tick - LAG, side).wait_recv()
-                tile_out(l, tick - LAG, side, True)
-                stage[lax.rem(tick, 2), side] = jnp.where(from_here, pick[side, place], land[side, lax.rem(tick + RING - LAG, RING)])
-
-            @pl.when(tick < LAG)
+            @pl.when(tick >= 1)
+            def _():
+                tile_copy(tick - 1, side).wait_recv()
+                tile_out(l, tick - 1, side, True)
+                stage[lax.rem(tick, 2), side] = jnp.where(from_here, pick[side, place], land[side, lax.rem(tick + RING - 1, RING)])
+
+            @pl.when(tick < 1)
             def _():
                 stage[lax.rem(tick, 2), side] = pick[side, place]
 
-        @pl.when(tick + 1 < TILES)
+        @pl.when(tick + 1 < TICKS)
         def _():
             pick_start(l, tick + 1)
 
         for side in range(2):
-            @pl.when(tick > LAG)
-            def _():
-                tile_out(l, tick - LAG - 1, side, False)
+            @pl.when(tick > 1)
+            def _():
+                tile_out(l, tick - 2, side, False)
 
             tile_copy(tick, side).start()
 
     def beat(l, k):
-        ring_step(l, k)
+        @pl.when(k < TICKS)
+        def _():
+            ring_step(l, k)
 
         @pl.when(k < HALF)
         def _():
-            own_copy(0, k + HALF).start()
-            own_copy(1, k).start()
+            late_copy(0, k).start()
+            late_copy(1, k).start()
 
         @pl.when((k >= HALF) & (k < HALF + PIECES))
         def _():
@@ -272,15 +286,15 @@
             relay_copy(0, k - HALF - PIECES).start()
             relay_copy(1, k - HALF - PIECES).start()
 
-    def ring_finish(l):
-        for side in range(2):
-            tile_out(l, jnp.int32(TICKS - LAG - 1), side, False)
-            for tick in range(TICKS - LAG, TICKS):
-                tile_copy(jnp.int32(tick), side).wait_recv()
-                tile_out(l, jnp.int32(tick), side, True)
-            for tick in range(TICKS - LAG, TICKS):
+    def ring_end(l):
+        for side in range(2):
+            tile_copy(jnp.int32(TICKS - 1), side).wait_recv()
+            tile_out(l, jnp.int32(TICKS - 1), side, True)
+
+    def ring_close(l):
+        for side in range(2):
+            for tick in range(TICKS - 2, TICKS):
                 tile_out(l, jnp.int32(tick), side, False)
-            for tick in range(TICKS - 2, TICKS):
                 tile_copy(jnp.int32(tick), side).wait_send()
 
     tok_in = pltpu.make_async_copy(tok_ref, blk.at[0], io_sem.at[0])
@@ -293,14 +307,14 @@
     fetch(jnp.int32(0), 1)
 
     barrier = pltpu.get_barrier_semaphore()
-    for dev in (left, right, mate):
+    for dev in (left, right, across, mate):
         pl.semaphore_signal(barrier, inc=1, device_id={'ep': dev}, device_id_type=MESH)
-    pl.semaphore_wait(barrier, 3)
+    pl.semaphore_wait(barrier, 4)
 
     tok_in.wait()
     for c in range(HALF):
-        own_copy(0, c).start()
-        own_copy(1, c + HALF).start()
+        for side in range(2):
+            lead_copy(side, c).start()
     for l in range(layers):
         for j in range(slots):
             for copy in mate_copies(l, j):
@@ -316,10 +330,14 @@
                 serves = jnp.where(map_ref[l, p] == expert, 0.0, serves)
             gates = jnp.sum(jnp.where(rbuf[l] == expert, gbuf[l], 0.0), axis=0, keepdims=True)
             at = slots * CORES * l + q % (slots * CORES)
-            cbuf[0, q // (slots * CORES), at:at + 1, :] = gates * serves
-    coef_copy(0).start()
-    coef_copy(1).start()
-    columns(0, 0, 0)
+            cbuf[q // (slots * CORES), at:at + 1, :] = gates * serves
+    for n in range(3):
+        coef_copy(n).start()
+    columns(0, cbuf[chip], cbuf[chip])
+    for l in range(layers):
+        _, origin, _, ringed, _, places = read_plan(map_ref, slot_ref, expert_ref, l, chips, CORES * slots, chip, core, slots)
+        sends = [ringed[m] & (origin[m] == chip) for m in range(2)]
+        inject_ref[l] = jnp.where(sends[0], places[0], jnp.where(sends[1], places[1], -1))
 
     @pl.loop(0, layers)
     def layer(l):
@@ -339,10 +357,9 @@
                 @pl.when(i == at)
                 def _():
                     for c in pieces:
-                        own_copy(0, c).wait_recv()
-                        forward_copy(0, c).start()
-                        own_copy(1, c + HALF).wait_recv()
-                        forward_copy(1, c).start()
+                        for side in range(2):
+                            lead_copy(side, c).wait_recv()
+                            forward_copy(side, c).start()
 
             @pl.when(i == 4)
             def _():
@@ -350,28 +367,21 @@
 
                 @pl.when(l == 0)
                 def _():
-                    coef_copy(0).wait_recv()
-                    coef_copy(2).start()
-                    coef_copy(1).wait_recv()
-                    columns(1, 1, 2)
-                    columns(2, 2, 1)
+                    await_bytes(cgot, co_recv)
+                    columns(1, cgot[0], cgot[1])
+                    columns(2, cgot[1], cgot[0])
+                    columns(3, cgot[2], cgot[2])
 
             @pl.when(i == 9)
             def _():
-                for c in range(HALF):
-                    for side in range(2):
-                        forward_copy(side, c).wait()
-
-                @pl.when(l == 0)
-                def _():
-                    coef_copy(2).wait_recv()
-                    columns(3, 3, 3)
+                for side in range(2):
+                    await_bytes(blk.at[3, whole_half(side)], fw_recv.at[side])
+                    await_bytes(blk.at[1, whole_half(side)], fw_send.at[side])
 
             @pl.when(i == 13)
             def _():
-                for c in range(HALF):
-                    own_copy(0, c + HALF).wait_recv()
-                    own_copy(1, c).wait_recv()
+                for side in range(2):
+                    await_bytes(blk.at[2, whole_half(1 - side)], la_recv.at[side])
 
             tick = jnp.where(i < FIRST + HALF, i - FIRST, HALF + 2 * (i - FIRST - HALF))
 
@@ -424,15 +434,14 @@
             def _():
                 fetch(n + 1, 1)
 
-        for c in range(CHUNKS):
-            own_copy(0, c).wait_send()
-            own_copy(1, c).wait_send()
-
-        @pl.loop(0, PIECES)
+        for side in range(2):
+            await_bytes(blk.at[0], ag_send.at[side])
+
+        ring_end(l)
+
         def merge(c):
             for side in range(2):
-                relay_copy(side, c).wait_recv()
-                at = sums(c + side * PIECES)
+                at = halves(c, side)
                 part[2, at] = part[2, at] + xin[side, sums(c)]
             for side in range(2):
                 @pl.when(l + 1 < layers)
@@ -443,52 +452,57 @@
                 def _():
                     sum_out(side, c).start()
 
-        ring_finish(l)
+        for side in range(2):
+            await_bytes(xin.at[side, pl.ds(0, (EARLY + 1) * (half_rows // PIECES))], xi_recv.at[side, 0])
+
+        pl.loop(0, EARLY + 1)(merge)
+
+        @pl.loop(EARLY + 1, PIECES)
+        def _(c):
+            for side in range(2):
+                relay_copy(side, c).wait_recv()
+            merge(c)
+
+        for side in range(2):
+            await_bytes(rdir.at[side], di_recv.at[side])
 
         @pl.when(l + 1 < layers)
         def _():
             @pl.loop(0, HALF)
             def finish(c):
                 for side in range(2):
-                    for p in range(PIECES // HALF):
-                        direct_copy(side, c * (PIECES // HALF) + p).wait_recv()
-                        merged_copy(side, c * (PIECES // HALF) + p).wait_recv()
+                    await_bytes(rmrg.at[side, rows(c)], mg_recv.at[side, c])
                     d = rows(c + side * HALF)
                     blk[0, d] = (part[0, d] + rdir[side, rows(c)] + rmrg[side, rows(c)]).astype(BF16)
                 for side in range(2):
-                    own_copy(side, c + side * HALF).start()
-
-            for c in range(PIECES):
-                for side in range(2):
-                    merged_copy(side, c).wait_send()
+                    lead_copy(side, c).start()
+
+            for side in range(2):
+                await_bytes(part.at[2, whole_half(side)], mg_send.at[side])
 
         @pl.when(l + 1 == layers)
         def _():
             @pl.loop(0, PIECES)
             def finish(c):
                 for side in range(2):
-                    direct_copy(side, c).wait_recv()
-                    d = sums(c + side * PIECES)
+                    d = halves(c, side)
                     part[0, d] = part[0, d] + rdir[side, sums(c)]
                 for side in range(2):
                     base_out(side, c).start()
 
-        for c in range(PIECES):
-            for side in range(2):
-                direct_copy(side, c).wait_send()
-                relay_copy(side, c).wait_send()
-
-    for c in range(PIECES):
-        for side in range(2):
-            sum_out(side, c).wait()
-            base_out(side, c).wait()
-    for n in range(3):
-        coef_copy(n).wait_send()
+        ring_close(l)
+        for side in range(2):
+            await_bytes(part.at[1, whole_half(side)], di_send.at[side])
+            await_bytes(part.at[3, whole_half(side)], xi_send.at[side])
+
+    for side in range(2):
+        await_bytes(part.at[2, whole_half(side)], sum_sem.at[side])
+        await_bytes(part.at[0, whole_half(side)], out_sem.at[side])
+    await_bytes(cgot, co_send)
     for l in range(layers):
-        pltpu.make_async_copy(arr_ref.at[l], far_ref.at[l], far_recv.at[l]).wait()
-        for j in range(slots):
-            for copy in mate_copies(l, j):
-                copy.wait_send()
+        await_bytes(far_ref.at[l], far_recv.at[l])
+    for n, ref in enumerate((pg_ref, pu_ref, pd_ref)):
+        await_bytes(ref, pw_send.at[n])
 
 
 def run_moe(group, old_map, move_slot, move_expert, routes, gates, tok, w_gate, w_up, w_down, sh_gate, sh_up, sh_down):
@@ -519,16 +533,18 @@
             pltpu.VMEM((n_rows, ffn), BF16),
             pltpu.VMEM(routes.shape, jnp.int32),
             pltpu.VMEM(gates.shape, F32),
-            pltpu.VMEM((chips, chips, layers * slots * CORES, n_rows), F32),
+            pltpu.VMEM((chips, layers * slots * CORES, n_rows), F32),
+            pltpu.VMEM((chips - 1, layers * slots * CORES, n_rows), F32),
             pltpu.VMEM((chips, n_rows, LANES), F32),
             pltpu.VMEM((n_rows, LANES), F32),
             pltpu.VMEM((2, CORES * slots, TILE, TILE), BF16),
             pltpu.VMEM((2, RING, TILE, TILE), BF16),
             pltpu.VMEM((2, 2, TILE, TILE), BF16),
-            dma((2, CHUNKS)), dma((2, CHUNKS)), dma((2, HALF)), dma((2, HALF)), dma((3,)), dma((3,)),
-            dma((layers, slots, 3)), dma((layers, slots, 3)),
-            dma((2, PIECES)), dma((2, PIECES)), dma((2, PIECES)), dma((2, PIECES)), dma((2, PIECES)), dma((2, PIECES)),
-            dma((2,)), dma((2,)), dma, dma((3,)), dma((2, PIECES)), dma((2, PIECES)),
+            pltpu.SMEM((layers,), jnp.int32),
+            dma((2,)), dma((2, HALF)), dma((2,)), dma((2,)), dma((2,)), dma, dma,
+            dma((3,)), dma((layers, slots, 3)),
+            dma((2,)), dma((2,)), dma((2,)), dma((2, PIECES - EARLY)), dma((2,)), dma((2, HALF)),
+            dma((2,)), dma((2,)), dma, dma((3,)), dma((2,)), dma((2,)),
             dma((2, 2)), dma((2, 2)), dma((2, RING)), dma((2, 2)), dma((2, 2)), dma((layers,)),
         ],
         compiler_params=pltpu.CompilerParams(collective_id=0, has_side_effects=True, vmem_limit_bytes=67043328),
@@ -558,8 +574,8 @@
                 ahead = lax.rem(goals[m] - origin[m] + chips, chips)
                 mode = jnp.where(here, jnp.where(near[m], NEAR, jnp.where(ringed[m], RINGED, KEEP)), mode)
                 pos = jnp.where(here, places[m], pos)
-                first = jnp.where(here, (ahead - 1) * LAG, first)
-                second = jnp.where(here, (chips - ahead - 1) * LAG, second)
+                first = jnp.where(here, ahead - 1, first)
+                second = jnp.where(here, chips - ahead - 1, second)
             table[l, j] = mode, pos, (first, second)
     jobs = [(l, j, n) for l in range(layers) for j in range(slots) for n in range(3)]
 
@@ -590,19 +606,22 @@
 
         @pl.when(mode == RINGED)
         def _():
-            for side in range(2):
-                start = starts[side] + 6 * n
-                for source, owner in ((arr_ref, core), (far_ref, 1 - core)):
-                    tall_at = 2 * TILE * (2 * owner + side)
-
-                    @pl.loop(0, 6)
-                    def _(t):
-                        if n == 2:
-                            r, c = TILE * (t // 2), tall_at + TILE * lax.rem(t, 2)
-                        else:
-                            r, c = tall_at + TILE * (t // 3), TILE * lax.rem(t, 3)
-                        spot = (pl.ds(pl.multiple_of(r, TILE), TILE), pl.ds(pl.multiple_of(c, TILE), TILE))
-                        pltpu.make_async_copy(source.at[l, side, start + t], buf.at[spot], sem).start()
+            across_ffn, across_half = wg_ref.shape[3] // TILE, PER // (wg_ref.shape[3] // TILE)
+            for source, owner in ((arr_ref, core), (far_ref, 1 - core)):
+                mine = across_half * TILE * owner
+
+                @pl.loop(0, PER)
+                def _(t):
+                    tile = PER * n + t
+                    one = tile < TICKS - starts[0]
+                    side = jnp.where(one, 0, 1)
+                    tick = jnp.where(one, tile + starts[0], TILES - 1 - tile + starts[1])
+                    if n == 2:
+                        r, c = TILE * (t // across_half), mine + TILE * lax.rem(t, across_half)
+                    else:
+                        r, c = mine + TILE * (t // across_ffn), TILE * lax.rem(t, across_ffn)
+                    spot = (pl.ds(pl.multiple_of(r, TILE), TILE), pl.ds(pl.multiple_of(c, TILE), TILE))
+                    pltpu.make_async_copy(source.at[l, side, tick], buf.at[spot], sem).start()
 
     def arrive(k):
         l, j, n, own, other, new, buf = parts(k)

time: 543 us -> 532 us (0.980)
  Pallas kernels: 515 us -> 504 us
    pallas_call x1, Pallas kernels: 488 us -> 477 us  [run_moe(): pl.pallas_call(functools.partial(moe_kernel, group), name='moe', out_shap...]
where the time goes in v6:
time: 532 us; the launch traced here: 531 us
  Pallas kernels  504 us (95%)
  waiting for transfers between devices  16.9 us (3%)
  other arithmetic  5.49 us (1%)
    pallas_call x1, Pallas kernels, run_moe(): pl.pallas_call(functools.partial(moe_kernel, group), name='moe', out_shap...  477 us
    pallas_call x1, Pallas kernels, run_place(): pl.pallas_call(functools.partial(place_kernel, group), name='place', out_...  27.5 us
    ppermute x1, waiting for transfers between devices, body(): lax.ppermute(first, 'ep', rightward)  16.9 us
  transfers between devices with their start and end apart: 2, of which 1 were waited for; matrix products, arithmetic and copies ran while one was open for 0% of the time, Pallas kernels for 5%

profile of v6, /device:TPU:112, one launch (start us, length us, event | category | flops | bytes accessed | tf_op | source)
XLA Modules:
  0.0 531.4 jit_solution(52177940631304892)
XLA Ops:
  0.6 477.0 %moe.1 = (f32[512,2048]{1,0:T(8,128)}, f32[256,2048]{1,0:T(8,128)}, f32[256,2048]{1,0:T(8,128)}, bf16[2,2,2048,768]{3,2,1,0:T(8,128)(2,1)}, bf16[2,2,2048,768]{3...) custom-call(s32[2,16]{1,0:T(2,128)} %map_ref.3, ...), custom_call_target="tpu_custom_call" | custom-call | flops 164282499072 | bytes 419430400 | tf_op jit(solution)/shard_map/moe/pallas_call | solution.py:517
  477.6 0.4 collective-permute-start.3
  478.1 2.9 collective-permute-start.4
  480.9 27.5 %place.1 = (bf16[2,2,2048,768]{3,2,1,0:T(8,128)(2,1)}, bf16[2,2,2048,768]{3,2,1,0:T(8,128)(2,1)}, bf16[2,2,768,2048]{3,2,1,0:T(8,128)(2,1)}, s32[2]{0:T(128)S(1)}) custom-call(s32[2,16]{1,0:T(2,128)} %map_ref.3, s32[2,2]{1,0:T(2,128)} %slot_ref.3, s32[2,2]{1,0:T(2,128)} %expert_ref.3, bf16[2,2,2048,768]{3,2,1,0:T(8,128)(2,1)} %wg_ref.3, ...), custom_call_target="tpu_custom_call" | custom-call | flops 20000000000 | bytes 80000000 | tf_op jit(solution)/shard_map/place/pallas_call | solution.py:652
  508.4 0.6 reduce_sum.9
  509.1 16.9 %collective-permute-done.3 = f32[256,2048]{1,0:T(8,128)S(1)} collective-permute-done((f32[256,2048]{1,0:T(8,128)}, f32[256,2048]{1,0:T(8,128)S(1)}, u32[]{:S(2)}, u32[]{:S(2)}) %collective-permute-start.3) | collective-permute-done | bytes 2097184 | tf_op jit(solution)/shard_map/ppermute | solution.py:700
  526.0 0.0 collective-permute-done.4
  526.0 0.0 copy-start.7
  526.0 0.0 copy-start.8
  526.0 0.0 copy-start.9
  526.0 0.0 copy-start.10
  526.0 4.9 fusion.4
  530.9 0.0 copy-done.7
  530.9 0.0 copy-done.8
  530.9 0.0 copy-done.9
  530.9 0.0 copy-done.10
  530.9 0.6 while.53
Async XLA Ops:
  477.6 48.4 %collective-permute-start.3 = (f32[256,2048]{1,0:T(8,128)}, f32[256,2048]{1,0:T(8,128)S(1)}, u32[]{:S(2)}, u32[]{:S(2)}) collective-permute-start(f32[256,2048]{1,0:T(8,128)} %get-tuple-element.316), channel_id=1, source_target_pairs={{0,2},{1,3},{2,4},{3,5},{4,6},{5,7},{6,0},{7,1},{8,10},{9,11},{10,... | collective-permute-start | bytes 6291464 | tf_op jit(solution)/shard_map/ppermute | solution.py:700
  478.1 47.9 %collective-permute-start.4 = (f32[256,2048]{1,0:T(8,128)}, f32[256,2048]{1,0:T(8,128)}, u32[]{:S(2)}, u32[]{:S(2)}) collective-permute-start(f32[256,2048]{1,0:T(8,128)} %get-tuple-element.317), channel_id=1, source_target_pairs={{0,6},{1,7},{2,0},{3,1},{4,2},{5,3},{6,4},{7,5},{8,14},{9,15},{10,... | collective-permute-start | bytes 6291464 | tf_op jit(solution)/shard_map/ppermute | solution.py:700
  526.0 4.9 copy-start.7
  526.0 4.9 copy-start.8
  526.0 4.9 copy-start.9
  526.0 4.9 copy-start.10
